TPU v7x, 512 devices: a whole 4x4x16 slice. The times are simulated.
512 devices in a mesh: cuts: 4 (over z_hi), fsdp: 128 (over y, x, z_lo, core).
Axes of the slice: x: 4, y: 4, z: 16 (z_hi: 4, z_lo: 4; z = z_hi * 4 + z_lo), core: 2. Of those that a mesh axis runs over, the one named last changes fastest.
Arguments:
- tokens: bfloat16 [65536, 8192], P(('cuts', 'fsdp')), may hold values from -240 to 240
- norm_gain: bfloat16 [8192], P('fsdp'), may hold values from 0.5 to 1.5
- gate_weight: bfloat16 [8192, 256], P('fsdp'), may hold values from -0.0625 to 0.0625
- up_weight: bfloat16 [8192, 256], P('fsdp'), may hold values from -0.0625 to 0.0625
- down_weight: bfloat16 [256, 8192], P(None, 'fsdp'), may hold values from -0.375 to 0.375
- slice_grads: float32 [4, 3, 8192, 256], P('cuts', None, 'fsdp'), may hold values from -6 to 6
Outputs:
- branch_out: bfloat16 [65536, 8192], P(('cuts', 'fsdp'))
- grad_mean: float32 [3, 8192, 256], P(None, 'fsdp')
All inputs are finite; a program needn't handle non-finite values.
Results may differ from a plain program's by a relative error of at most 0.0065.
Values may be sent and summed in bfloat16 or wider, within the bound.
No kernel may reach another device: no remote copies, remote signals or barrier semaphores. Data moves between devices by JAX's collectives and lax.ppermute only.
A program may use at most 64 MiB of HBM per device.

v0:
```python
import functools
import itertools

import jax
import jax.numpy as jnp
from jax import lax
from jax.experimental import pallas as pl
from jax.experimental.pallas import tpu as pltpu
from jax.sharding import Mesh
from jax.sharding import PartitionSpec as P

AXES = ("c", "y", "x", "z", "k")
FSDP = AXES[1:]
SUM_DIMS = (((1,), (0,)), ((), ()))
ROW_DIMS = (((1,), (1,)), ((), ()))
VMEM = pl.BlockSpec(memory_space=pltpu.VMEM)
SMEM = pl.BlockSpec(memory_space=pltpu.SMEM)
ANY = pl.BlockSpec(memory_space=pl.ANY)
HBM = pl.BlockSpec(memory_space=pltpu.HBM)
EPS = 1e-05
LANES = 128
SHARE, HALF, WIDE = 512, 256, 256
HALVES = ((0, 1), (3, 2))
EARLY = ((0, 0), (0, 1), (1, 0), (3, 1), (1, 1), (3, 0))
LATE = ((2, 1), (2, 0))
ORDER = EARLY + LATE


def moved(value, sizes, to):
    index = lambda at: functools.reduce(lambda i, s: i * s[1] + s[0], zip(at, sizes), 0)
    pairs = [(index(at), index(to(*at))) for at in itertools.product(*map(range, sizes))]
    return lax.ppermute(value, AXES, pairs)


def over_cuts(m):
    return lambda c, y, x, z, k: (c ^ m, y, x, z, k)


def other_core(c, y, x, z, k):
    return (c, y, x, z, 1 - k)


def first_axis(m):
    return lambda c, y, x, z, k: (c, y ^ (m * k), x ^ (m * (1 - k)), z, k)


def second_axis(m):
    return lambda c, y, x, z, k: (c, y ^ (m * (1 - k)), x ^ (m * k), z, k)


def pack_kernel(gain_hbm, gate_hbm, up_hbm, down_hbm, out_ref, gain_ref, gate_ref, up_ref, sems):
    f = gate_hbm.shape[1]
    copies = [
        pltpu.make_async_copy(a, b, sems.at[n])
        for n, (a, b) in enumerate(
            [
                (gain_hbm, gain_ref),
                (gate_hbm, gate_ref),
                (up_hbm, up_ref),
                (down_hbm, out_ref.at[:, 2 * f :]),
            ]
        )
    ]
    for copy in copies:
        copy.start()
    for copy in copies:
        copy.wait()
    rows = gate_hbm.shape[0]
    at = lambda d: lax.broadcasted_iota(jnp.int32, (rows, rows), d)
    gain = jnp.where(at(0) == at(1), gain_ref[...].astype(jnp.float32), 0.0)
    gain = jnp.sum(gain, axis=1, keepdims=True)
    gate = (gate_ref[...].astype(jnp.float32) * gain).astype(out_ref.dtype)
    up = (up_ref[...].astype(jnp.float32) * gain).astype(out_ref.dtype)
    h = f // 2
    for k in range(2):
        for n, w in enumerate((gate, up)):
            out_ref[:, (2 * k + n) * h : (2 * k + n + 1) * h] = w[:, k * h : (k + 1) * h]


def pack(gain, gate, up, down):
    rows, f = gate.shape
    return pl.pallas_call(
        pack_kernel,
        out_shape=jax.ShapeDtypeStruct((rows, 3 * f), gate.dtype),
        in_specs=[ANY] * 4,
        out_specs=VMEM,
        scratch_shapes=[
            pltpu.VMEM((1, rows), gate.dtype),
            pltpu.VMEM((rows, f), gate.dtype),
            pltpu.VMEM((rows, f), gate.dtype),
            pltpu.SemaphoreType.DMA((4,)),
        ],
        name="pack",
    )(gain[None, :], gate, up, down)


def load_tokens(steps, at_ref, toks, tok_ref, sems):
    rows = toks[0].shape[0]
    copies = []
    for s, (a, half) in enumerate(steps):
        for i, j in enumerate(HALVES[half]):
            start = pl.multiple_of(at_ref[4 * a + j], SHARE)
            for who in range(2):
                copies.append(
                    pltpu.make_async_copy(
                        toks[who].at[:, pl.ds(start, SHARE)],
                        tok_ref.at[s, i, who * rows : (who + 1) * rows, :],
                        sems.at[s, i, who],
                    )
                )
    for copy in copies:
        copy.start()
    return copies


def add_piece(total, square, tok, gate_up):
    total += lax.dot_general(tok, gate_up, SUM_DIMS, preferred_element_type=jnp.float32)
    for l in range(0, SHARE, LANES):
        t = tok[:, l : l + LANES].astype(jnp.float32)
        square += t * t
    return total, square


def early_kernel(at_ref, *refs):
    n = len(EARLY)
    toks, pieces, (out_ref, down_ref, tok_ref, sems) = refs[:2], refs[2 : 2 + n], refs[2 + n :]
    copies = load_tokens(EARLY, at_ref, toks, tok_ref, sems)
    for s in range(n):
        down_ref[s] = pieces[s][:, SHARE:, :]
    total = jnp.zeros((2 * toks[0].shape[0], WIDE), jnp.float32)
    square = jnp.zeros((2 * toks[0].shape[0], LANES), jnp.float32)
    for s, i in itertools.product(range(n), range(2)):
        for who in range(2):
            copies[4 * s + 2 * i + who].wait()
        total, square = add_piece(total, square, tok_ref[s, i], pieces[s][i, :SHARE, :])
    out_ref[:, :WIDE] = total
    out_ref[:, WIDE:] = square


def late_kernel(at_ref, before_ref, *refs):
    n = len(LATE)
    toks, pieces, (mine_ref, send_ref, tok_ref, sems) = refs[:2], refs[2 : 2 + n], refs[2 + n :]
    rows = toks[0].shape[0]
    copies = load_tokens(LATE, at_ref, toks, tok_ref, sems)
    for part, (s, i) in enumerate(itertools.product(range(n), range(2))):
        send_ref[part * HALF : (part + 1) * HALF, :] = pieces[s][i, SHARE:, :]
    total, square = before_ref[:, :WIDE], before_ref[:, WIDE:]
    for s, i in itertools.product(range(n), range(2)):
        for who in range(2):
            copies[4 * s + 2 * i + who].wait()
        total, square = add_piece(total, square, tok_ref[s, i], pieces[s][i, :SHARE, :])
    mean = jnp.sum(square, axis=1, keepdims=True) / (2 * len(ORDER) * SHARE)
    total = total * lax.rsqrt(mean + EPS)
    gate, up = total[:, : WIDE // 2], total[:, WIDE // 2 :]
    hidden = (gate / (1.0 + jnp.exp(-gate)) * up).astype(jnp.bfloat16)
    mine_ref[...] = hidden[:rows]
    send_ref[2 * n * HALF :, : WIDE // 2] = hidden[rows:]
    send_ref[2 * n * HALF :, WIDE // 2 :] = hidden[:rows]


def sums_params(n):
    return dict(
        compiler_params=pltpu.CompilerParams(vmem_limit_bytes=8 * 2**20),
        cost_estimate=pl.CostEstimate(flops=n * 2**30, bytes_accessed=n * 2**20, transcendentals=0),
    )


def token_scratch(n, rows):
    return [
        pltpu.VMEM((n, 2, 2 * rows, SHARE), jnp.bfloat16),
        pltpu.SemaphoreType.DMA((n, 2, 2)),
    ]


def early_sums(at, tokens, pieces):
    n, rows = len(EARLY), tokens[0].shape[0]
    return pl.pallas_call(
        early_kernel,
        out_shape=[
            jax.ShapeDtypeStruct((2 * rows, WIDE + LANES), jnp.float32),
            jax.ShapeDtypeStruct((n, 2, HALF, WIDE), jnp.bfloat16),
        ],
        in_specs=[SMEM] + [HBM] * 2 + [VMEM] * n,
        out_specs=[VMEM, VMEM],
        scratch_shapes=token_scratch(n, rows),
        name="early",
        **sums_params(n),
    )(at, *tokens, *[pieces[s] for s in EARLY])


def late_sums(at, before, tokens, pieces):
    n, rows = len(LATE), tokens[0].shape[0]
    return pl.pallas_call(
        late_kernel,
        out_shape=[
            jax.ShapeDtypeStruct((rows, WIDE // 2), jnp.bfloat16),
            jax.ShapeDtypeStruct((2 * n * HALF + rows, WIDE), jnp.bfloat16),
        ],
        in_specs=[SMEM, VMEM] + [HBM] * 2 + [VMEM] * n,
        out_specs=[VMEM, VMEM],
        scratch_shapes=token_scratch(n, rows),
        name="late",
        **sums_params(n),
    )(at, before, *tokens, *[pieces[s] for s in LATE])


def down_kernel(at_ref, mine_ref, early_ref, late_ref, *refs):
    n = len(ORDER)
    own, (out_ref, out_held, out_sems) = refs[:n], refs[n:]
    mine, theirs = mine_ref[...], late_ref[2 * len(LATE) * HALF :, : WIDE // 2]
    hidden = jnp.where(
        at_ref[48] == 0,
        jnp.concatenate([mine, theirs], axis=1),
        jnp.concatenate([theirs, mine], axis=1),
    )
    copies = []
    for slot, (s, i, who) in enumerate(itertools.product(range(n), range(2), range(2))):
        a, half = ORDER[s]
        if who == 0:
            rows = own[s][i, SHARE:, :]
        elif s < len(EARLY):
            rows = early_ref[s, i]
        else:
            part = 2 * (s - len(EARLY)) + i
            rows = late_ref[part * HALF : (part + 1) * HALF, :]
        out = lax.dot_general(hidden, rows, ROW_DIMS, preferred_element_type=jnp.float32)
        out_held[slot] = out.astype(out_held.dtype)
        start = pl.multiple_of(at_ref[16 + 16 * who + 4 * a + HALVES[half][i]], HALF)
        copy = pltpu.make_async_copy(
            out_held.at[slot], out_ref.at[:, pl.ds(start, HALF)], out_sems.at[slot]
        )
        copy.start()
        copies.append(copy)
    for copy in copies:
        copy.wait()


def down(at, mine, early, late, own, tokens):
    n = len(ORDER)
    rows = tokens.shape[0]
    return pl.pallas_call(
        down_kernel,
        out_shape=jax.ShapeDtypeStruct(tokens.shape, jnp.bfloat16),
        in_specs=[SMEM] + [VMEM] * (n + 3),
        out_specs=HBM,
        scratch_shapes=[
            pltpu.VMEM((4 * n, rows, HALF), jnp.bfloat16),
            pltpu.SemaphoreType.DMA((4 * n,)),
        ],
        compiler_params=pltpu.CompilerParams(vmem_limit_bytes=8 * 2**20),
        name="down",
    )(at, mine, early, late, *[own[s] for s in ORDER])


def per_device(sizes, tokens, norm_gain, gate_weight, up_weight, down_weight, slice_grads):
    move = lambda value, to: moved(value, sizes, to)
    y, x, k = lax.axis_index("y"), lax.axis_index("x"), lax.axis_index("k")
    packed = pack(norm_gain, gate_weight, up_weight, down_weight.T)
    near = lax.all_gather(packed, ("z", "k"), axis=0, tiled=True)
    near = jnp.concatenate(
        [
            lax.dynamic_slice(near, (0, k * WIDE), (SHARE, WIDE)),
            lax.dynamic_slice(near, (k * HALF, 2 * WIDE), (HALF, WIDE)),
        ]
    )
    near, grads = lax.optimization_barrier((near, slice_grads[0]))
    mine = grads.astype(jnp.bfloat16)
    line = {m: move(near, first_axis(m)) for m in (1, 3, 2)}
    line[0] = near
    far = move(mine, over_cuts(1))
    both_tokens = (tokens, move(tokens, other_core))

    own = {}
    for h in range(2):
        own[0, h] = jnp.stack([line[j] for j in HALVES[h]])
    own[1, 0] = move(own[0, 0], second_axis(1))
    own[3, 1] = move(own[0, 1], second_axis(3))
    own[1, 1] = move(own[0, 1], second_axis(1))
    own[3, 0] = move(own[0, 0], second_axis(3))
    own[2, 0] = move(own[1, 0], second_axis(3))
    own[2, 1] = move(own[3, 1], second_axis(1))

    a, j = jnp.arange(16) // 4, jnp.arange(16) % 4
    place = lambda core: (y ^ jnp.where(core == 0, a, j)) * 4 + (x ^ jnp.where(core == 0, j, a))
    at = jnp.concatenate(
        [
            place(k) * SHARE,
            place(k) * SHARE + k * HALF,
            place(1 - k) * SHARE + (1 - k) * HALF,
            k[None],
        ]
    ).astype(jnp.int32)

    total, early = early_sums(at, both_tokens, own)
    early = move(early, other_core)
    pair = (mine.astype(jnp.float32) + far.astype(jnp.float32)).astype(jnp.bfloat16)
    rest = move(pair, over_cuts(3))
    grad_mean = (pair.astype(jnp.float32) + rest.astype(jnp.float32)) / sizes[0]
    mine_hidden, late = late_sums(at, total, both_tokens, own)
    late = move(late, other_core)
    branch = down(at, mine_hidden, early, late, own, tokens)
    return branch, grad_mean


def solution(mesh):
    cuts = mesh.shape["cuts"]
    sizes = (cuts, 4, 4, 4, 2)
    finer = Mesh(mesh.devices.reshape(sizes), AXES)
    in_specs = (
        P(AXES, None),
        P(FSDP),
        P(FSDP, None),
        P(FSDP, None),
        P(None, FSDP),
        P("c", None, FSDP, None),
    )
    out_specs = (P(AXES, None), P(None, FSDP, None))

    def body(*args):
        return per_device(sizes, *args)

    return jax.shard_map(
        body, mesh=finer, in_specs=in_specs, out_specs=out_specs, check_vma=False
    )
```

profile of v0, /device:TPU:1, one launch (start us, length us, event | category | flops | bytes accessed | tf_op | source)
XLA Modules:
  0.0 111.8 jit_solution(660609867929797107)
XLA Ops:
  0.6 8.8 %collective-permute-start = (bf16[128,8192]{1,0:T(8,128)(2,1)}, bf16[128,8192]{1,0:T(8,128)(2,1)}, u32[]{:S(2)}, u32[]{:S(2)}) collective-permute-start(bf16[128,8192]{1,0:T(8,128)(2,1)} %refs_0_.3), channel_id=1, source_target_pairs={{0,1},{1,0},{2,3},{3,2},{4,5},{5,4},{6,7},{7,6},{8,9},{9,8},{10,11... | collective-permute-start | bytes 6291464 | tf_op jit(solution)/shard_map/ppermute | solution.py:32
  9.4 1.6 %pack.1 = bf16[64,768]{1,0:T(8,128)(2,1)} custom-call(bf16[1,64]{1,0:T(2,128)(2,1)} %bitcast.15, bf16[64,256]{1,0:T(8,128)(2,1)} %gate_hbm.1, bf16[64,256]{1,0:T(8,128)(2,1)} %up_hbm.1, bf16[64,256]{1,0:T(8,128)(2,1)} %bitcast.14), custom_call_target="tpu_custom_call" | custom-call | tf_op jit(solution)/shard_map/pack/pallas_call | solution.py:82
  11.0 16.3 %all_gather.3 = bf16[512,768]{1,0:T(8,128)(2,1)S(1)} all-gather(bf16[64,768]{1,0:T(8,128)(2,1)} %pack.1), channel_id=1, replica_groups=mesh['c'=4,'y'=4,'x'=4,'z'=4,'k'=2] {'z','k'}, dimensions={0}, use_global_device_ids=true | all-gather | bytes 884736 | tf_op jit(solution)/shard_map/all_gather | solution.py:259
  27.4 1.9 %collective-permute-start.2 = (bf16[768,256]{1,0:T(8,128)(2,1)S(1)}, bf16[768,256]{1,0:T(8,128)(2,1)S(1)}, u32[]{:S(2)}, u32[]{:S(2)}) collective-permute-start(bf16[768,256]{1,0:T(8,128)(2,1)S(1)} %pad_maximum_fusion.2), channel_id=1, source_target_pairs={{0,24},{1,97},{2,26},{3,99},{4,28},{5,101},{6,30},{7,103},{8,16},{... | collective-permute-start | bytes 1179656 | tf_op jit(solution)/shard_map/ppermute | solution.py:32
  29.3 1.9 %collective-permute-start.3 = (bf16[768,256]{1,0:T(8,128)(2,1)S(1)}, bf16[768,256]{1,0:T(8,128)(2,1)S(1)}, u32[]{:S(2)}, u32[]{:S(2)}) collective-permute-start(bf16[768,256]{1,0:T(8,128)(2,1)S(1)} %pad_maximum_fusion.2), channel_id=1, source_target_pairs={{0,16},{1,65},{2,18},{3,67},{4,20},{5,69},{6,22},{7,71},{8,24},{9,... | collective-permute-start | bytes 1179656 | tf_op jit(solution)/shard_map/ppermute | solution.py:32
  31.2 5.1 %collective-permute-start.1 = (bf16[768,256]{1,0:T(8,128)(2,1)S(1)}, bf16[768,256]{1,0:T(8,128)(2,1)S(1)}, u32[]{:S(2)}, u32[]{:S(2)}) collective-permute-start(bf16[768,256]{1,0:T(8,128)(2,1)S(1)} %pad_maximum_fusion.2), channel_id=1, source_target_pairs={{0,8},{1,33},{2,10},{3,35},{4,12},{5,37},{6,14},{7,39},{8,0},{9,41... | collective-permute-start | bytes 1179656 | tf_op jit(solution)/shard_map/ppermute | solution.py:32
  36.4 5.2 %collective-permute-done.2 = bf16[768,256]{1,0:T(8,128)(2,1)S(1)} collective-permute-done((bf16[768,256]{1,0:T(8,128)(2,1)S(1)}, bf16[768,256]{1,0:T(8,128)(2,1)S(1)}, u32[]{:S(2)}, u32[]{:S(2)}) %collective-permute-start.2) | collective-permute-done | bytes 393248 | tf_op jit(solution)/shard_map/ppermute | solution.py:32
  41.6 0.0 collective-permute-done.3
  41.6 0.1 pad_maximum_fusion.1.refs_3_.refs_1_
  41.7 1.9 %collective-permute-start.5 = (bf16[2,768,256]{2,1,0:T(8,128)(2,1)S(1)}, bf16[2,768,256]{2,1,0:T(8,128)(2,1)S(1)}, u32[]{:S(2)}, u32[]{:S(2)}) collective-permute-start(bf16[2,768,256]{2,1,0:T(8,128)(2,1)S(1)} %pad_maximum_fusion.1.refs_3_.refs_1_), channel_id=1, source_target_pairs={{0,96},{1,25},{2,98},{3,27},{4,100},{5,29},{6,102},{7,31},{8,104},... | collective-permute-start | bytes 2359304 | tf_op jit(solution)/shard_map/ppermute | solution.py:32
  43.6 0.5 collective-permute-done.1
  44.1 0.1 pad_maximum_fusion.refs_2_.refs_0_
  44.2 1.9 %collective-permute-start.4 = (bf16[2,768,256]{2,1,0:T(8,128)(2,1)S(1)}, bf16[2,768,256]{2,1,0:T(8,128)(2,1)S(1)}, u32[]{:S(2)}, u32[]{:S(2)}) collective-permute-start(bf16[2,768,256]{2,1,0:T(8,128)(2,1)S(1)} %pad_maximum_fusion.refs_2_.refs_0_), channel_id=1, source_target_pairs={{0,32},{1,9},{2,34},{3,11},{4,36},{5,13},{6,38},{7,15},{8,40},{9,1... | collective-permute-start | bytes 2359304 | tf_op jit(solution)/shard_map/ppermute | solution.py:32
  46.1 3.4 %collective-permute-start.6 = (bf16[2,768,256]{2,1,0:T(8,128)(2,1)S(1)}, bf16[2,768,256]{2,1,0:T(8,128)(2,1)}, u32[]{:S(2)}, u32[]{:S(2)}) collective-permute-start(bf16[2,768,256]{2,1,0:T(8,128)(2,1)S(1)} %pad_maximum_fusion.1.refs_3_.refs_1_), channel_id=1, source_target_pairs={{0,32},{1,9},{2,34},{3,11},{4,36},{5,13},{6,38},{7,15},{8,40},{9,1... | collective-permute-start | bytes 2359304 | tf_op jit(solution)/shard_map/ppermute | solution.py:32
  49.5 4.1 %collective-permute-start.7 = (bf16[2,768,256]{2,1,0:T(8,128)(2,1)S(1)}, bf16[2,768,256]{2,1,0:T(8,128)(2,1)}, u32[]{:S(2)}, u32[]{:S(2)}) collective-permute-start(bf16[2,768,256]{2,1,0:T(8,128)(2,1)S(1)} %pad_maximum_fusion.refs_2_.refs_0_), channel_id=1, source_target_pairs={{0,96},{1,25},{2,98},{3,27},{4,100},{5,29},{6,102},{7,31},{8,104},... | collective-permute-start | bytes 2359304 | tf_op jit(solution)/shard_map/ppermute | solution.py:32
  53.6 0.1 pad_add_fusion.at_ref
  53.7 2.2 %collective-permute-done.5.refs_5_.refs_3_ = bf16[2,768,256]{2,1,0:T(8,128)(2,1)S(1)} collective-permute-done((bf16[2,768,256]{2,1,0:T(8,128)(2,1)S(1)}, bf16[2,768,256]{2,1,0:T(8,128)(2,1)S(1)}, u32[]{:S(2)}, u32[]{:S(2)}) %collective-permute-start.5) | collective-permute-done | bytes 786464 | tf_op jit(solution)/shard_map/ppermute | solution.py:32
  55.9 1.9 %collective-permute-start.8 = (bf16[2,768,256]{2,1,0:T(8,128)(2,1)S(1)}, bf16[2,768,256]{2,1,0:T(8,128)(2,1)S(1)}, u32[]{:S(2)}, u32[]{:S(2)}) collective-permute-start(bf16[2,768,256]{2,1,0:T(8,128)(2,1)S(1)} %collective-permute-done.5.refs_5_.refs_3_), channel_id=1, source_target_pairs={{0,32},{1,9},{2,34},{3,11},{4,36},{5,13},{6,38},{7,15},{8,40},{9,1... | collective-permute-start | bytes 2359304 | tf_op jit(solution)/shard_map/ppermute | solution.py:32
  57.9 0.0 collective-permute-done.4.refs_4_.refs_2_
  57.9 3.6 %collective-permute-start.9 = (bf16[2,768,256]{2,1,0:T(8,128)(2,1)S(1)}, bf16[2,768,256]{2,1,0:T(8,128)(2,1)S(1)}, u32[]{:S(2)}, u32[]{:S(2)}) collective-permute-start(bf16[2,768,256]{2,1,0:T(8,128)(2,1)S(1)} %collective-permute-done.4.refs_4_.refs_2_), channel_id=1, source_target_pairs={{0,96},{1,25},{2,98},{3,27},{4,100},{5,29},{6,102},{7,31},{8,104},... | collective-permute-start | bytes 2359304 | tf_op jit(solution)/shard_map/ppermute | solution.py:32
  61.4 4.3 %collective-permute-done.6.refs_6_.refs_4_ = bf16[2,768,256]{2,1,0:T(8,128)(2,1)} collective-permute-done((bf16[2,768,256]{2,1,0:T(8,128)(2,1)S(1)}, bf16[2,768,256]{2,1,0:T(8,128)(2,1)}, u32[]{:S(2)}, u32[]{:S(2)}) %collective-permute-start.6) | collective-permute-done | bytes 786464 | tf_op jit(solution)/shard_map/ppermute | solution.py:32
  65.8 0.0 collective-permute-done.7.refs_7_.refs_5_
  65.8 0.0 collective-permute-done.refs_1_
  65.8 0.0 copy-start
  65.8 1.6 %copy-done = bf16[128,8192]{1,0:T(8,128)(2,1)S(1)} copy-done((bf16[128,8192]{1,0:T(8,128)(2,1)S(1)}, bf16[128,8192]{1,0:T(8,128)(2,1)}, u32[]{:S(2)}) %copy-start) | copy-done | bytes 2097176
  67.4 0.0 copy-start.2
  67.4 0.0 copy-start.1
  67.4 5.0 %early.1 = (f32[256,384]{1,0:T(8,128)S(1)}, bf16[6,2,256,256]{3,2,1,0:T(8,128)(2,1)S(1)}) custom-call(s32[49]{0:T(128)S(1)} %pad_add_fusion.at_ref, bf16[128,8192]{1,0:T(8,128)(2,1)S(1)} %copy-done, bf16[128,8192]{1,0:T(8,128)(2,1)} %collective-permute-done.refs_1_, bf16[2,768,256]{2,1,0:T(8,128)(2,1)S(1)} %pad_maximum_fusion.refs_2_.refs_0_, ...), custom_call_target="tpu_custom_call" | custom-call | flops 6442450944 | bytes 6291456 | tf_op jit(solution)/shard_map/early/pallas_call | solution.py:177
  72.4 4.1 %collective-permute-start.10 = (bf16[6,2,256,256]{3,2,1,0:T(8,128)(2,1)S(1)}, bf16[6,2,256,256]{3,2,1,0:T(8,128)(2,1)S(1)}, u32[]{:S(2)}, u32[]{:S(2)}) collective-permute-start(bf16[6,2,256,256]{3,2,1,0:T(8,128)(2,1)S(1)} %get-tuple-element.11), channel_id=1, source_target_pairs={{0,1},{1,0},{2,3},{3,2},{4,5},{5,4},{6,7},{7,6},{8,9},{9,8},{10,11... | collective-permute-start | bytes 4718600 | tf_op jit(solution)/shard_map/ppermute | solution.py:32
  76.4 0.0 copy-done.2
  76.5 7.1 %collective-permute-start.12 = (bf16[3,64,256]{2,1,0:T(8,128)(2,1)S(1)}, bf16[3,64,256]{2,1,0:T(8,128)(2,1)S(1)}, u32[]{:S(2)}, u32[]{:S(2)}) collective-permute-start(bf16[3,64,256]{2,1,0:T(8,128)(2,1)S(1)} %convert_element_type.18), channel_id=1, source_target_pairs={{0,128},{1,129},{2,130},{3,131},{4,132},{5,133},{6,134},{7,135},{8... | collective-permute-start | bytes 294920 | tf_op jit(solution)/shard_map/ppermute | solution.py:32
  83.6 0.0 collective-permute-done.8.refs_2_.refs_6_
  83.6 0.0 collective-permute-done.9.refs_3_.refs_7_
  83.6 0.0 copy-done.1
  83.6 2.5 %late.1 = (bf16[128,128]{1,0:T(8,128)(2,1)S(1)}, bf16[1152,256]{1,0:T(8,128)(2,1)S(1)}) custom-call(s32[49]{0:T(128)S(1)} %pad_add_fusion.at_ref, f32[256,384]{1,0:T(8,128)S(1)} %get-tuple-element.9.before_ref, bf16[128,8192]{1,0:T(8,128)(2,1)S(1)} %copy-done.1, bf16[128,8192]{1,0:T(8,128)(2,1)} %collective-permute-done.refs_1_, ...), custom_call_target="tpu_custom_call" | custom-call | flops 2147483648 | bytes 2097152 | tf_op jit(solution)/shard_map/late/pallas_call | solution.py:193
  86.1 2.2 %collective-permute-start.11 = (bf16[1152,256]{1,0:T(8,128)(2,1)S(1)}, bf16[1152,256]{1,0:T(8,128)(2,1)S(1)}, u32[]{:S(2)}, u32[]{:S(2)}) collective-permute-start(bf16[1152,256]{1,0:T(8,128)(2,1)S(1)} %get-tuple-element.12), channel_id=1, source_target_pairs={{0,1},{1,0},{2,3},{3,2},{4,5},{5,4},{6,7},{7,6},{8,9},{9,8},{10,11... | collective-permute-start | bytes 1769480 | tf_op jit(solution)/shard_map/ppermute | solution.py:32
  88.3 4.8 %collective-permute-done.12 = bf16[3,64,256]{2,1,0:T(8,128)(2,1)S(1)} collective-permute-done((bf16[3,64,256]{2,1,0:T(8,128)(2,1)S(1)}, bf16[3,64,256]{2,1,0:T(8,128)(2,1)S(1)}, u32[]{:S(2)}, u32[]{:S(2)}) %collective-permute-start.12) | collective-permute-done | bytes 98336 | tf_op jit(solution)/shard_map/ppermute | solution.py:32
  93.2 6.7 %collective-permute-start.13 = (bf16[3,64,256]{2,1,0:T(8,128)(2,1)S(1)}, bf16[3,64,256]{2,1,0:T(8,128)(2,1)S(1)}, u32[]{:S(2)}, u32[]{:S(2)}) collective-permute-start(bf16[3,64,256]{2,1,0:T(8,128)(2,1)S(1)} %add_convert_fusion), channel_id=1, source_target_pairs={{0,384},{1,385},{2,386},{3,387},{4,388},{5,389},{6,390},{7,391},{8... | collective-permute-start | bytes 294920 | tf_op jit(solution)/shard_map/ppermute | solution.py:32
  99.9 7.3 %collective-permute-done.13 = bf16[3,64,256]{2,1,0:T(8,128)(2,1)S(1)} collective-permute-done((bf16[3,64,256]{2,1,0:T(8,128)(2,1)S(1)}, bf16[3,64,256]{2,1,0:T(8,128)(2,1)S(1)}, u32[]{:S(2)}, u32[]{:S(2)}) %collective-permute-start.13) | collective-permute-done | bytes 98336 | tf_op jit(solution)/shard_map/ppermute | solution.py:32
  107.2 0.7 add_multiply_fusion
  107.9 0.0 collective-permute-done.11.late_ref
  107.9 0.0 collective-permute-done.10.early_ref
  107.9 3.8 %down.1 = bf16[128,8192]{1,0:T(8,128)(2,1)} custom-call(s32[49]{0:T(128)S(1)} %pad_add_fusion.at_ref, bf16[128,128]{1,0:T(8,128)(2,1)S(1)} %get-tuple-element.10.mine_ref, bf16[6,2,256,256]{3,2,1,0:T(8,128)(2,1)S(1)} %collective-permute-done.10.early_ref, bf16[1152,256]{1,0:T(8,128)(2,1)S(1)} %collective-permute-done.11.late_ref, ...), custom_call_target="tpu_custom_call" | custom-call | tf_op jit(solution)/shard_map/down/pallas_call | solution.py:241
  (7 shorter events, 0.1 us)
Async XLA Ops:
  0.6 65.1 %collective-permute-start = (bf16[128,8192]{1,0:T(8,128)(2,1)}, bf16[128,8192]{1,0:T(8,128)(2,1)}, u32[]{:S(2)}, u32[]{:S(2)}) collective-permute-start(bf16[128,8192]{1,0:T(8,128)(2,1)} %refs_0_.3), channel_id=1, source_target_pairs={{0,1},{1,0},{2,3},{3,2},{4,5},{5,4},{6,7},{7,6},{8,9},{9,8},{10,11... | collective-permute-start | bytes 6291464 | tf_op jit(solution)/shard_map/ppermute | solution.py:32
  27.4 14.2 %collective-permute-start.2 = (bf16[768,256]{1,0:T(8,128)(2,1)S(1)}, bf16[768,256]{1,0:T(8,128)(2,1)S(1)}, u32[]{:S(2)}, u32[]{:S(2)}) collective-permute-start(bf16[768,256]{1,0:T(8,128)(2,1)S(1)} %pad_maximum_fusion.2), channel_id=1, source_target_pairs={{0,24},{1,97},{2,26},{3,99},{4,28},{5,101},{6,30},{7,103},{8,16},{... | collective-permute-start | bytes 1179656 | tf_op jit(solution)/shard_map/ppermute | solution.py:32
  29.3 12.3 %collective-permute-start.3 = (bf16[768,256]{1,0:T(8,128)(2,1)S(1)}, bf16[768,256]{1,0:T(8,128)(2,1)S(1)}, u32[]{:S(2)}, u32[]{:S(2)}) collective-permute-start(bf16[768,256]{1,0:T(8,128)(2,1)S(1)} %pad_maximum_fusion.2), channel_id=1, source_target_pairs={{0,16},{1,65},{2,18},{3,67},{4,20},{5,69},{6,22},{7,71},{8,24},{9,... | collective-permute-start | bytes 1179656 | tf_op jit(solution)/shard_map/ppermute | solution.py:32
  31.2 12.9 %collective-permute-start.1 = (bf16[768,256]{1,0:T(8,128)(2,1)S(1)}, bf16[768,256]{1,0:T(8,128)(2,1)S(1)}, u32[]{:S(2)}, u32[]{:S(2)}) collective-permute-start(bf16[768,256]{1,0:T(8,128)(2,1)S(1)} %pad_maximum_fusion.2), channel_id=1, source_target_pairs={{0,8},{1,33},{2,10},{3,35},{4,12},{5,37},{6,14},{7,39},{8,0},{9,41... | collective-permute-start | bytes 1179656 | tf_op jit(solution)/shard_map/ppermute | solution.py:32
  41.7 14.2 %collective-permute-start.5 = (bf16[2,768,256]{2,1,0:T(8,128)(2,1)S(1)}, bf16[2,768,256]{2,1,0:T(8,128)(2,1)S(1)}, u32[]{:S(2)}, u32[]{:S(2)}) collective-permute-start(bf16[2,768,256]{2,1,0:T(8,128)(2,1)S(1)} %pad_maximum_fusion.1.refs_3_.refs_1_), channel_id=1, source_target_pairs={{0,96},{1,25},{2,98},{3,27},{4,100},{5,29},{6,102},{7,31},{8,104},... | collective-permute-start | bytes 2359304 | tf_op jit(solution)/shard_map/ppermute | solution.py:32
  44.2 13.7 %collective-permute-start.4 = (bf16[2,768,256]{2,1,0:T(8,128)(2,1)S(1)}, bf16[2,768,256]{2,1,0:T(8,128)(2,1)S(1)}, u32[]{:S(2)}, u32[]{:S(2)}) collective-permute-start(bf16[2,768,256]{2,1,0:T(8,128)(2,1)S(1)} %pad_maximum_fusion.refs_2_.refs_0_), channel_id=1, source_target_pairs={{0,32},{1,9},{2,34},{3,11},{4,36},{5,13},{6,38},{7,15},{8,40},{9,1... | collective-permute-start | bytes 2359304 | tf_op jit(solution)/shard_map/ppermute | solution.py:32
  46.1 19.6 %collective-permute-start.6 = (bf16[2,768,256]{2,1,0:T(8,128)(2,1)S(1)}, bf16[2,768,256]{2,1,0:T(8,128)(2,1)}, u32[]{:S(2)}, u32[]{:S(2)}) collective-permute-start(bf16[2,768,256]{2,1,0:T(8,128)(2,1)S(1)} %pad_maximum_fusion.1.refs_3_.refs_1_), channel_id=1, source_target_pairs={{0,32},{1,9},{2,34},{3,11},{4,36},{5,13},{6,38},{7,15},{8,40},{9,1... | collective-permute-start | bytes 2359304 | tf_op jit(solution)/shard_map/ppermute | solution.py:32
  49.5 16.3 %collective-permute-start.7 = (bf16[2,768,256]{2,1,0:T(8,128)(2,1)S(1)}, bf16[2,768,256]{2,1,0:T(8,128)(2,1)}, u32[]{:S(2)}, u32[]{:S(2)}) collective-permute-start(bf16[2,768,256]{2,1,0:T(8,128)(2,1)S(1)} %pad_maximum_fusion.refs_2_.refs_0_), channel_id=1, source_target_pairs={{0,96},{1,25},{2,98},{3,27},{4,100},{5,29},{6,102},{7,31},{8,104},... | collective-permute-start | bytes 2359304 | tf_op jit(solution)/shard_map/ppermute | solution.py:32
  55.9 27.6 %collective-permute-start.8 = (bf16[2,768,256]{2,1,0:T(8,128)(2,1)S(1)}, bf16[2,768,256]{2,1,0:T(8,128)(2,1)S(1)}, u32[]{:S(2)}, u32[]{:S(2)}) collective-permute-start(bf16[2,768,256]{2,1,0:T(8,128)(2,1)S(1)} %collective-permute-done.5.refs_5_.refs_3_), channel_id=1, source_target_pairs={{0,32},{1,9},{2,34},{3,11},{4,36},{5,13},{6,38},{7,15},{8,40},{9,1... | collective-permute-start | bytes 2359304 | tf_op jit(solution)/shard_map/ppermute | solution.py:32
  57.9 25.7 %collective-permute-start.9 = (bf16[2,768,256]{2,1,0:T(8,128)(2,1)S(1)}, bf16[2,768,256]{2,1,0:T(8,128)(2,1)S(1)}, u32[]{:S(2)}, u32[]{:S(2)}) collective-permute-start(bf16[2,768,256]{2,1,0:T(8,128)(2,1)S(1)} %collective-permute-done.4.refs_4_.refs_2_), channel_id=1, source_target_pairs={{0,96},{1,25},{2,98},{3,27},{4,100},{5,29},{6,102},{7,31},{8,104},... | collective-permute-start | bytes 2359304 | tf_op jit(solution)/shard_map/ppermute | solution.py:32
  65.8 1.6 %copy-start = (bf16[128,8192]{1,0:T(8,128)(2,1)S(1)}, bf16[128,8192]{1,0:T(8,128)(2,1)}, u32[]{:S(2)}) copy-start(bf16[128,8192]{1,0:T(8,128)(2,1)} %refs_0_.3) | copy-start | bytes 6291460
  67.4 9.1 %copy-start.2 = (f32[1,3,64,256]{3,2,1,0:T(8,128)S(1)}, f32[1,3,64,256]{3,2,1,0:T(8,128)}, u32[]{:S(2)}) copy-start(f32[1,3,64,256]{3,2,1,0:T(8,128)} %param.11) | copy-start | bytes 589828
  67.4 16.3 %copy-start.1 = (bf16[128,8192]{1,0:T(8,128)(2,1)S(1)}, bf16[128,8192]{1,0:T(8,128)(2,1)}, u32[]{:S(2)}) copy-start(bf16[128,8192]{1,0:T(8,128)(2,1)} %refs_0_.3) | copy-start | bytes 6291460
  72.4 35.6 %collective-permute-start.10 = (bf16[6,2,256,256]{3,2,1,0:T(8,128)(2,1)S(1)}, bf16[6,2,256,256]{3,2,1,0:T(8,128)(2,1)S(1)}, u32[]{:S(2)}, u32[]{:S(2)}) collective-permute-start(bf16[6,2,256,256]{3,2,1,0:T(8,128)(2,1)S(1)} %get-tuple-element.11), channel_id=1, source_target_pairs={{0,1},{1,0},{2,3},{3,2},{4,5},{5,4},{6,7},{7,6},{8,9},{9,8},{10,11... | collective-permute-start | bytes 4718600 | tf_op jit(solution)/shard_map/ppermute | solution.py:32
  76.5 16.7 %collective-permute-start.12 = (bf16[3,64,256]{2,1,0:T(8,128)(2,1)S(1)}, bf16[3,64,256]{2,1,0:T(8,128)(2,1)S(1)}, u32[]{:S(2)}, u32[]{:S(2)}) collective-permute-start(bf16[3,64,256]{2,1,0:T(8,128)(2,1)S(1)} %convert_element_type.18), channel_id=1, source_target_pairs={{0,128},{1,129},{2,130},{3,131},{4,132},{5,133},{6,134},{7,135},{8... | collective-permute-start | bytes 294920 | tf_op jit(solution)/shard_map/ppermute | solution.py:32
  86.1 21.8 %collective-permute-start.11 = (bf16[1152,256]{1,0:T(8,128)(2,1)S(1)}, bf16[1152,256]{1,0:T(8,128)(2,1)S(1)}, u32[]{:S(2)}, u32[]{:S(2)}) collective-permute-start(bf16[1152,256]{1,0:T(8,128)(2,1)S(1)} %get-tuple-element.12), channel_id=1, source_target_pairs={{0,1},{1,0},{2,3},{3,2},{4,5},{5,4},{6,7},{7,6},{8,9},{9,8},{10,11... | collective-permute-start | bytes 1769480 | tf_op jit(solution)/shard_map/ppermute | solution.py:32
  93.2 14.0 %collective-permute-start.13 = (bf16[3,64,256]{2,1,0:T(8,128)(2,1)S(1)}, bf16[3,64,256]{2,1,0:T(8,128)(2,1)S(1)}, u32[]{:S(2)}, u32[]{:S(2)}) collective-permute-start(bf16[3,64,256]{2,1,0:T(8,128)(2,1)S(1)} %add_convert_fusion), channel_id=1, source_target_pairs={{0,384},{1,385},{2,386},{3,387},{4,388},{5,389},{6,390},{7,391},{8... | collective-permute-start | bytes 294920 | tf_op jit(solution)/shard_map/ppermute | solution.py:32
where the time goes:
time: 112 us
  starting transfers between devices  54.6 us (49%)
  waiting for transfers between devices  24.5 us (22%)
  blocking collectives  16.3 us (15%)
  Pallas kernels  12.9 us (12%)
  local copies, waits for them, and re-layouts  1.63 us (1%)
    ppermute x14, starting transfers between devices, moved(): return lax.ppermute(value, AXES, pairs)  54.6 us
    ppermute x14, waiting for transfers between devices, moved(): return lax.ppermute(value, AXES, pairs)  24.5 us
    all_gather x1, blocking collectives, per_device(): near = lax.all_gather(packed, ('z', 'k'), axis=0, tiled=True)  16.3 us
    pallas_call x1, Pallas kernels, early_sums(): pl.pallas_call(early_kernel, out_shape=[jax.ShapeDtypeStruct((2 * rows, W...  4.99 us
    pallas_call x1, Pallas kernels, down(): pl.pallas_call(down_kernel, out_shape=jax.ShapeDtypeStruct(tokens.shape,...  3.84 us
    pallas_call x1, Pallas kernels, late_sums(): pl.pallas_call(late_kernel, out_shape=[jax.ShapeDtypeStruct((rows, WIDE /...  2.48 us
  transfers between devices with their start and end apart: 14, of which 6 were waited for; matrix products, arithmetic and copies ran while one was open for 1% of the time, Pallas kernels for 8%

commit v1 on v0

--- a/solution.py
+++ b/solution.py
@@ -94,7 +94,7 @@
     )(gain[None, :], gate, up, down)
 
 
-def load_tokens(steps, at_ref, toks, tok_ref, sems):
+def token_copies(steps, at_ref, toks, tok_ref, sems):
     rows = toks[0].shape[0]
     copies = []
     for s, (a, half) in enumerate(steps):
@@ -108,8 +108,6 @@
                         sems.at[s, i, who],
                     )
                 )
-    for copy in copies:
-        copy.start()
     return copies
 
 
@@ -123,8 +121,12 @@
 
 def early_kernel(at_ref, *refs):
     n = len(EARLY)
-    toks, pieces, (out_ref, down_ref, tok_ref, sems) = refs[:2], refs[2 : 2 + n], refs[2 + n :]
-    copies = load_tokens(EARLY, at_ref, toks, tok_ref, sems)
+    toks, pieces = refs[:2], refs[2 : 2 + n]
+    out_ref, down_ref, late_tok_ref, tok_ref, sems, late_sems = refs[2 + n :]
+    copies = token_copies(EARLY, at_ref, toks, tok_ref, sems)
+    late_copies = token_copies(LATE, at_ref, toks, late_tok_ref, late_sems)
+    for copy in copies + late_copies:
+        copy.start()
     for s in range(n):
         down_ref[s] = pieces[s][:, SHARE:, :]
     total = jnp.zeros((2 * toks[0].shape[0], WIDE), jnp.float32)
@@ -135,19 +137,18 @@
         total, square = add_piece(total, square, tok_ref[s, i], pieces[s][i, :SHARE, :])
     out_ref[:, :WIDE] = total
     out_ref[:, WIDE:] = square
-
-
-def late_kernel(at_ref, before_ref, *refs):
+    for copy in late_copies:
+        copy.wait()
+
+
+def late_kernel(before_ref, tok_ref, *refs):
     n = len(LATE)
-    toks, pieces, (mine_ref, send_ref, tok_ref, sems) = refs[:2], refs[2 : 2 + n], refs[2 + n :]
-    rows = toks[0].shape[0]
-    copies = load_tokens(LATE, at_ref, toks, tok_ref, sems)
+    pieces, (mine_ref, send_ref) = refs[:n], refs[n:]
+    rows = mine_ref.shape[0]
     for part, (s, i) in enumerate(itertools.product(range(n), range(2))):
         send_ref[part * HALF : (part + 1) * HALF, :] = pieces[s][i, SHARE:, :]
     total, square = before_ref[:, :WIDE], before_ref[:, WIDE:]
     for s, i in itertools.product(range(n), range(2)):
-        for who in range(2):
-            copies[4 * s + 2 * i + who].wait()
         total, square = add_piece(total, square, tok_ref[s, i], pieces[s][i, :SHARE, :])
     mean = jnp.sum(square, axis=1, keepdims=True) / (2 * len(ORDER) * SHARE)
     total = total * lax.rsqrt(mean + EPS)
@@ -165,43 +166,40 @@
     )
 
 
-def token_scratch(n, rows):
-    return [
-        pltpu.VMEM((n, 2, 2 * rows, SHARE), jnp.bfloat16),
-        pltpu.SemaphoreType.DMA((n, 2, 2)),
-    ]
-
-
 def early_sums(at, tokens, pieces):
-    n, rows = len(EARLY), tokens[0].shape[0]
+    n, m, rows = len(EARLY), len(LATE), tokens[0].shape[0]
     return pl.pallas_call(
         early_kernel,
         out_shape=[
             jax.ShapeDtypeStruct((2 * rows, WIDE + LANES), jnp.float32),
             jax.ShapeDtypeStruct((n, 2, HALF, WIDE), jnp.bfloat16),
+            jax.ShapeDtypeStruct((m, 2, 2 * rows, SHARE), jnp.bfloat16),
         ],
         in_specs=[SMEM] + [HBM] * 2 + [VMEM] * n,
-        out_specs=[VMEM, VMEM],
-        scratch_shapes=token_scratch(n, rows),
+        out_specs=[VMEM, VMEM, VMEM],
+        scratch_shapes=[
+            pltpu.VMEM((n, 2, 2 * rows, SHARE), jnp.bfloat16),
+            pltpu.SemaphoreType.DMA((n, 2, 2)),
+            pltpu.SemaphoreType.DMA((m, 2, 2)),
+        ],
         name="early",
         **sums_params(n),
     )(at, *tokens, *[pieces[s] for s in EARLY])
 
 
-def late_sums(at, before, tokens, pieces):
-    n, rows = len(LATE), tokens[0].shape[0]
+def late_sums(before, late_tokens, rows, pieces):
+    n = len(LATE)
     return pl.pallas_call(
         late_kernel,
         out_shape=[
             jax.ShapeDtypeStruct((rows, WIDE // 2), jnp.bfloat16),
             jax.ShapeDtypeStruct((2 * n * HALF + rows, WIDE), jnp.bfloat16),
         ],
-        in_specs=[SMEM, VMEM] + [HBM] * 2 + [VMEM] * n,
+        in_specs=[VMEM] * (2 + n),
         out_specs=[VMEM, VMEM],
-        scratch_shapes=token_scratch(n, rows),
         name="late",
         **sums_params(n),
-    )(at, before, *tokens, *[pieces[s] for s in LATE])
+    )(before, late_tokens, *[pieces[s] for s in LATE])
 
 
 def down_kernel(at_ref, mine_ref, early_ref, late_ref, *refs):
@@ -291,12 +289,12 @@
         ]
     ).astype(jnp.int32)
 
-    total, early = early_sums(at, both_tokens, own)
+    total, early, late_tokens = early_sums(at, both_tokens, own)
     early = move(early, other_core)
     pair = (mine.astype(jnp.float32) + far.astype(jnp.float32)).astype(jnp.bfloat16)
     rest = move(pair, over_cuts(3))
     grad_mean = (pair.astype(jnp.float32) + rest.astype(jnp.float32)) / sizes[0]
-    mine_hidden, late = late_sums(at, total, both_tokens, own)
+    mine_hidden, late = late_sums(total, late_tokens, tokens.shape[0], own)
     late = move(late, other_core)
     branch = down(at, mine_hidden, early, late, own, tokens)
     return branch, grad_mean

time: 112 us -> 112 us (level)
  Pallas kernels: 12.9 us -> 10.9 us
  waiting for transfers between devices: 24.5 us -> 26.5 us
    ppermute x14, waiting for transfers between devices: 24.5 us -> 26.5 us  [moved(): return lax.ppermute(value, AXES, pairs)]
    pallas_call x1, Pallas kernels: 2.48 us -> 0.51 us  [late_sums(): pl.pallas_call(late_kernel, out_shape=[jax.ShapeDtypeStruct((rows, WIDE /...]
  transfers between devices with their start and end apart: 14 -> 14, of which waited for: 6 -> 6; matrix products, arithmetic and copies ran while one was open for 1% -> 1% of each run, Pallas kernels for 8% -> 6%
where the time goes in v1:
time: 112 us
  starting transfers between devices  54.6 us (49%)
  waiting for transfers between devices  26.5 us (24%)
  blocking collectives  16.3 us (15%)
  Pallas kernels  10.9 us (10%)
  local copies, waits for them, and re-layouts  1.63 us (1%)
    ppermute x14, starting transfers between devices, moved(): return lax.ppermute(value, AXES, pairs)  54.6 us
    ppermute x14, waiting for transfers between devices, moved(): return lax.ppermute(value, AXES, pairs)  26.5 us
    all_gather x1, blocking collectives, per_device(): near = lax.all_gather(packed, ('z', 'k'), axis=0, tiled=True)  16.3 us
    pallas_call x1, Pallas kernels, early_sums(): pl.pallas_call(early_kernel, out_shape=[jax.ShapeDtypeStruct((2 * rows, W...  4.96 us
    pallas_call x1, Pallas kernels, down(): pl.pallas_call(down_kernel, out_shape=jax.ShapeDtypeStruct(tokens.shape,...  3.84 us
  transfers between devices with their start and end apart: 14, of which 6 were waited for; matrix products, arithmetic and copies ran while one was open for 1% of the time, Pallas kernels for 6%

profile of v1, /device:TPU:1, one launch (start us, length us, event | category | flops | bytes accessed | tf_op | source)
XLA Modules:
  0.0 111.8 jit_solution(6454271768441066671)
XLA Ops:
  0.6 8.8 %collective-permute-start = (bf16[128,8192]{1,0:T(8,128)(2,1)}, bf16[128,8192]{1,0:T(8,128)(2,1)}, u32[]{:S(2)}, u32[]{:S(2)}) collective-permute-start(bf16[128,8192]{1,0:T(8,128)(2,1)} %refs_0_.1), channel_id=1, source_target_pairs={{0,1},{1,0},{2,3},{3,2},{4,5},{5,4},{6,7},{7,6},{8,9},{9,8},{10,11... | collective-permute-start | bytes 6291464 | tf_op jit(solution)/shard_map/ppermute | solution.py:32
  9.4 1.6 %pack.1 = bf16[64,768]{1,0:T(8,128)(2,1)} custom-call(bf16[1,64]{1,0:T(2,128)(2,1)} %bitcast.15, bf16[64,256]{1,0:T(8,128)(2,1)} %gate_hbm.1, bf16[64,256]{1,0:T(8,128)(2,1)} %up_hbm.1, bf16[64,256]{1,0:T(8,128)(2,1)} %bitcast.14), custom_call_target="tpu_custom_call" | custom-call | tf_op jit(solution)/shard_map/pack/pallas_call | solution.py:82
  11.0 16.3 %all_gather.3 = bf16[512,768]{1,0:T(8,128)(2,1)S(1)} all-gather(bf16[64,768]{1,0:T(8,128)(2,1)} %pack.1), channel_id=1, replica_groups=mesh['c'=4,'y'=4,'x'=4,'z'=4,'k'=2] {'z','k'}, dimensions={0}, use_global_device_ids=true | all-gather | bytes 884736 | tf_op jit(solution)/shard_map/all_gather | solution.py:257
  27.4 1.9 %collective-permute-start.2 = (bf16[768,256]{1,0:T(8,128)(2,1)S(1)}, bf16[768,256]{1,0:T(8,128)(2,1)S(1)}, u32[]{:S(2)}, u32[]{:S(2)}) collective-permute-start(bf16[768,256]{1,0:T(8,128)(2,1)S(1)} %pad_maximum_fusion.2), channel_id=1, source_target_pairs={{0,24},{1,97},{2,26},{3,99},{4,28},{5,101},{6,30},{7,103},{8,16},{... | collective-permute-start | bytes 1179656 | tf_op jit(solution)/shard_map/ppermute | solution.py:32
  29.3 1.9 %collective-permute-start.3 = (bf16[768,256]{1,0:T(8,128)(2,1)S(1)}, bf16[768,256]{1,0:T(8,128)(2,1)S(1)}, u32[]{:S(2)}, u32[]{:S(2)}) collective-permute-start(bf16[768,256]{1,0:T(8,128)(2,1)S(1)} %pad_maximum_fusion.2), channel_id=1, source_target_pairs={{0,16},{1,65},{2,18},{3,67},{4,20},{5,69},{6,22},{7,71},{8,24},{9,... | collective-permute-start | bytes 1179656 | tf_op jit(solution)/shard_map/ppermute | solution.py:32
  31.2 5.1 %collective-permute-start.1 = (bf16[768,256]{1,0:T(8,128)(2,1)S(1)}, bf16[768,256]{1,0:T(8,128)(2,1)S(1)}, u32[]{:S(2)}, u32[]{:S(2)}) collective-permute-start(bf16[768,256]{1,0:T(8,128)(2,1)S(1)} %pad_maximum_fusion.2), channel_id=1, source_target_pairs={{0,8},{1,33},{2,10},{3,35},{4,12},{5,37},{6,14},{7,39},{8,0},{9,41... | collective-permute-start | bytes 1179656 | tf_op jit(solution)/shard_map/ppermute | solution.py:32
  36.4 5.2 %collective-permute-done.2 = bf16[768,256]{1,0:T(8,128)(2,1)S(1)} collective-permute-done((bf16[768,256]{1,0:T(8,128)(2,1)S(1)}, bf16[768,256]{1,0:T(8,128)(2,1)S(1)}, u32[]{:S(2)}, u32[]{:S(2)}) %collective-permute-start.2) | collective-permute-done | bytes 393248 | tf_op jit(solution)/shard_map/ppermute | solution.py:32
  41.6 0.0 collective-permute-done.3
  41.6 0.1 pad_maximum_fusion.1.refs_3_.refs_1_
  41.7 1.9 %collective-permute-start.5 = (bf16[2,768,256]{2,1,0:T(8,128)(2,1)S(1)}, bf16[2,768,256]{2,1,0:T(8,128)(2,1)S(1)}, u32[]{:S(2)}, u32[]{:S(2)}) collective-permute-start(bf16[2,768,256]{2,1,0:T(8,128)(2,1)S(1)} %pad_maximum_fusion.1.refs_3_.refs_1_), channel_id=1, source_target_pairs={{0,96},{1,25},{2,98},{3,27},{4,100},{5,29},{6,102},{7,31},{8,104},... | collective-permute-start | bytes 2359304 | tf_op jit(solution)/shard_map/ppermute | solution.py:32
  43.6 0.5 collective-permute-done.1
  44.1 0.1 pad_maximum_fusion.refs_2_.refs_0_
  44.2 1.9 %collective-permute-start.4 = (bf16[2,768,256]{2,1,0:T(8,128)(2,1)S(1)}, bf16[2,768,256]{2,1,0:T(8,128)(2,1)S(1)}, u32[]{:S(2)}, u32[]{:S(2)}) collective-permute-start(bf16[2,768,256]{2,1,0:T(8,128)(2,1)S(1)} %pad_maximum_fusion.refs_2_.refs_0_), channel_id=1, source_target_pairs={{0,32},{1,9},{2,34},{3,11},{4,36},{5,13},{6,38},{7,15},{8,40},{9,1... | collective-permute-start | bytes 2359304 | tf_op jit(solution)/shard_map/ppermute | solution.py:32
  46.1 3.4 %collective-permute-start.6 = (bf16[2,768,256]{2,1,0:T(8,128)(2,1)S(1)}, bf16[2,768,256]{2,1,0:T(8,128)(2,1)}, u32[]{:S(2)}, u32[]{:S(2)}) collective-permute-start(bf16[2,768,256]{2,1,0:T(8,128)(2,1)S(1)} %pad_maximum_fusion.1.refs_3_.refs_1_), channel_id=1, source_target_pairs={{0,32},{1,9},{2,34},{3,11},{4,36},{5,13},{6,38},{7,15},{8,40},{9,1... | collective-permute-start | bytes 2359304 | tf_op jit(solution)/shard_map/ppermute | solution.py:32
  49.5 4.1 %collective-permute-start.7 = (bf16[2,768,256]{2,1,0:T(8,128)(2,1)S(1)}, bf16[2,768,256]{2,1,0:T(8,128)(2,1)}, u32[]{:S(2)}, u32[]{:S(2)}) collective-permute-start(bf16[2,768,256]{2,1,0:T(8,128)(2,1)S(1)} %pad_maximum_fusion.refs_2_.refs_0_), channel_id=1, source_target_pairs={{0,96},{1,25},{2,98},{3,27},{4,100},{5,29},{6,102},{7,31},{8,104},... | collective-permute-start | bytes 2359304 | tf_op jit(solution)/shard_map/ppermute | solution.py:32
  53.6 0.1 pad_add_fusion.at_ref
  53.7 2.2 %collective-permute-done.5.refs_5_.refs_3_ = bf16[2,768,256]{2,1,0:T(8,128)(2,1)S(1)} collective-permute-done((bf16[2,768,256]{2,1,0:T(8,128)(2,1)S(1)}, bf16[2,768,256]{2,1,0:T(8,128)(2,1)S(1)}, u32[]{:S(2)}, u32[]{:S(2)}) %collective-permute-start.5) | collective-permute-done | bytes 786464 | tf_op jit(solution)/shard_map/ppermute | solution.py:32
  55.9 1.9 %collective-permute-start.8 = (bf16[2,768,256]{2,1,0:T(8,128)(2,1)S(1)}, bf16[2,768,256]{2,1,0:T(8,128)(2,1)S(1)}, u32[]{:S(2)}, u32[]{:S(2)}) collective-permute-start(bf16[2,768,256]{2,1,0:T(8,128)(2,1)S(1)} %collective-permute-done.5.refs_5_.refs_3_), channel_id=1, source_target_pairs={{0,32},{1,9},{2,34},{3,11},{4,36},{5,13},{6,38},{7,15},{8,40},{9,1... | collective-permute-start | bytes 2359304 | tf_op jit(solution)/shard_map/ppermute | solution.py:32
  57.9 0.0 collective-permute-done.4.refs_4_.refs_2_
  57.9 3.6 %collective-permute-start.9 = (bf16[2,768,256]{2,1,0:T(8,128)(2,1)S(1)}, bf16[2,768,256]{2,1,0:T(8,128)(2,1)S(1)}, u32[]{:S(2)}, u32[]{:S(2)}) collective-permute-start(bf16[2,768,256]{2,1,0:T(8,128)(2,1)S(1)} %collective-permute-done.4.refs_4_.refs_2_), channel_id=1, source_target_pairs={{0,96},{1,25},{2,98},{3,27},{4,100},{5,29},{6,102},{7,31},{8,104},... | collective-permute-start | bytes 2359304 | tf_op jit(solution)/shard_map/ppermute | solution.py:32
  61.4 4.3 %collective-permute-done.6.refs_6_.refs_4_ = bf16[2,768,256]{2,1,0:T(8,128)(2,1)} collective-permute-done((bf16[2,768,256]{2,1,0:T(8,128)(2,1)S(1)}, bf16[2,768,256]{2,1,0:T(8,128)(2,1)}, u32[]{:S(2)}, u32[]{:S(2)}) %collective-permute-start.6) | collective-permute-done | bytes 786464 | tf_op jit(solution)/shard_map/ppermute | solution.py:32
  65.8 0.0 collective-permute-done.7.refs_7_.refs_5_
  65.8 0.0 collective-permute-done.refs_1_
  65.8 0.0 copy-start
  65.8 1.6 %copy-done = bf16[128,8192]{1,0:T(8,128)(2,1)S(1)} copy-done((bf16[128,8192]{1,0:T(8,128)(2,1)S(1)}, bf16[128,8192]{1,0:T(8,128)(2,1)}, u32[]{:S(2)}) %copy-start) | copy-done | bytes 2097176
  67.4 0.0 copy-start.1
  67.4 5.0 %early.1 = (f32[256,384]{1,0:T(8,128)S(1)}, bf16[6,2,256,256]{3,2,1,0:T(8,128)(2,1)S(1)}, bf16[2,2,256,512]{3,2,1,0:T(8,128)(2,1)S(1)}) custom-call(s32[49]{0:T(128)S(1)} %pad_add_fusion.at_ref, bf16[128,8192]{1,0:T(8,128)(2,1)S(1)} %copy-done, bf16[128,8192]{1,0:T(8,128)(2,1)} %collective-permute-done.refs_1_, ...), custom_call_target="tpu_custom_call" | custom-call | flops 6442450944 | bytes 6291456 | tf_op jit(solution)/shard_map/early/pallas_call | solution.py:171
  72.3 4.1 %collective-permute-start.10 = (bf16[6,2,256,256]{3,2,1,0:T(8,128)(2,1)S(1)}, bf16[6,2,256,256]{3,2,1,0:T(8,128)(2,1)S(1)}, u32[]{:S(2)}, u32[]{:S(2)}) collective-permute-start(bf16[6,2,256,256]{3,2,1,0:T(8,128)(2,1)S(1)} %get-tuple-element.13), channel_id=1, source_target_pairs={{0,1},{1,0},{2,3},{3,2},{4,5},{5,4},{6,7},{7,6},{8,9},{9,8},{10,11... | collective-permute-start | bytes 4718600 | tf_op jit(solution)/shard_map/ppermute | solution.py:32
  76.4 0.0 copy-done.1
  76.4 7.1 %collective-permute-start.12 = (bf16[3,64,256]{2,1,0:T(8,128)(2,1)S(1)}, bf16[3,64,256]{2,1,0:T(8,128)(2,1)S(1)}, u32[]{:S(2)}, u32[]{:S(2)}) collective-permute-start(bf16[3,64,256]{2,1,0:T(8,128)(2,1)S(1)} %convert_element_type.18), channel_id=1, source_target_pairs={{0,128},{1,129},{2,130},{3,131},{4,132},{5,133},{6,134},{7,135},{8... | collective-permute-start | bytes 294920 | tf_op jit(solution)/shard_map/ppermute | solution.py:32
  83.6 0.0 collective-permute-done.8.refs_0_.refs_6_
  83.6 0.0 collective-permute-done.9.refs_1_.refs_7_
  83.6 0.5 late.1
  84.1 2.2 %collective-permute-start.11 = (bf16[1152,256]{1,0:T(8,128)(2,1)S(1)}, bf16[1152,256]{1,0:T(8,128)(2,1)S(1)}, u32[]{:S(2)}, u32[]{:S(2)}) collective-permute-start(bf16[1152,256]{1,0:T(8,128)(2,1)S(1)} %get-tuple-element.14), channel_id=1, source_target_pairs={{0,1},{1,0},{2,3},{3,2},{4,5},{5,4},{6,7},{7,6},{8,9},{9,8},{10,11... | collective-permute-start | bytes 1769480 | tf_op jit(solution)/shard_map/ppermute | solution.py:32
  86.3 6.8 %collective-permute-done.12 = bf16[3,64,256]{2,1,0:T(8,128)(2,1)S(1)} collective-permute-done((bf16[3,64,256]{2,1,0:T(8,128)(2,1)S(1)}, bf16[3,64,256]{2,1,0:T(8,128)(2,1)S(1)}, u32[]{:S(2)}, u32[]{:S(2)}) %collective-permute-start.12) | collective-permute-done | bytes 98336 | tf_op jit(solution)/shard_map/ppermute | solution.py:32
  93.2 6.7 %collective-permute-start.13 = (bf16[3,64,256]{2,1,0:T(8,128)(2,1)S(1)}, bf16[3,64,256]{2,1,0:T(8,128)(2,1)S(1)}, u32[]{:S(2)}, u32[]{:S(2)}) collective-permute-start(bf16[3,64,256]{2,1,0:T(8,128)(2,1)S(1)} %add_convert_fusion), channel_id=1, source_target_pairs={{0,384},{1,385},{2,386},{3,387},{4,388},{5,389},{6,390},{7,391},{8... | collective-permute-start | bytes 294920 | tf_op jit(solution)/shard_map/ppermute | solution.py:32
  99.8 7.3 %collective-permute-done.13 = bf16[3,64,256]{2,1,0:T(8,128)(2,1)S(1)} collective-permute-done((bf16[3,64,256]{2,1,0:T(8,128)(2,1)S(1)}, bf16[3,64,256]{2,1,0:T(8,128)(2,1)S(1)}, u32[]{:S(2)}, u32[]{:S(2)}) %collective-permute-start.13) | collective-permute-done | bytes 98336 | tf_op jit(solution)/shard_map/ppermute | solution.py:32
  107.2 0.7 add_multiply_fusion
  107.9 0.0 collective-permute-done.11.late_ref
  107.9 0.0 collective-permute-done.10.early_ref
  107.9 3.8 %down.1 = bf16[128,8192]{1,0:T(8,128)(2,1)} custom-call(s32[49]{0:T(128)S(1)} %pad_add_fusion.at_ref, bf16[128,128]{1,0:T(8,128)(2,1)S(1)} %get-tuple-element.12.mine_ref, bf16[6,2,256,256]{3,2,1,0:T(8,128)(2,1)S(1)} %collective-permute-done.10.early_ref, bf16[1152,256]{1,0:T(8,128)(2,1)S(1)} %collective-permute-done.11.late_ref, ...), custom_call_target="tpu_custom_call" | custom-call | tf_op jit(solution)/shard_map/down/pallas_call | solution.py:239
  (7 shorter events, 0.1 us)
Async XLA Ops:
  0.6 65.1 %collective-permute-start = (bf16[128,8192]{1,0:T(8,128)(2,1)}, bf16[128,8192]{1,0:T(8,128)(2,1)}, u32[]{:S(2)}, u32[]{:S(2)}) collective-permute-start(bf16[128,8192]{1,0:T(8,128)(2,1)} %refs_0_.1), channel_id=1, source_target_pairs={{0,1},{1,0},{2,3},{3,2},{4,5},{5,4},{6,7},{7,6},{8,9},{9,8},{10,11... | collective-permute-start | bytes 6291464 | tf_op jit(solution)/shard_map/ppermute | solution.py:32
  27.4 14.2 %collective-permute-start.2 = (bf16[768,256]{1,0:T(8,128)(2,1)S(1)}, bf16[768,256]{1,0:T(8,128)(2,1)S(1)}, u32[]{:S(2)}, u32[]{:S(2)}) collective-permute-start(bf16[768,256]{1,0:T(8,128)(2,1)S(1)} %pad_maximum_fusion.2), channel_id=1, source_target_pairs={{0,24},{1,97},{2,26},{3,99},{4,28},{5,101},{6,30},{7,103},{8,16},{... | collective-permute-start | bytes 1179656 | tf_op jit(solution)/shard_map/ppermute | solution.py:32
  29.3 12.3 %collective-permute-start.3 = (bf16[768,256]{1,0:T(8,128)(2,1)S(1)}, bf16[768,256]{1,0:T(8,128)(2,1)S(1)}, u32[]{:S(2)}, u32[]{:S(2)}) collective-permute-start(bf16[768,256]{1,0:T(8,128)(2,1)S(1)} %pad_maximum_fusion.2), channel_id=1, source_target_pairs={{0,16},{1,65},{2,18},{3,67},{4,20},{5,69},{6,22},{7,71},{8,24},{9,... | collective-permute-start | bytes 1179656 | tf_op jit(solution)/shard_map/ppermute | solution.py:32
  31.2 12.9 %collective-permute-start.1 = (bf16[768,256]{1,0:T(8,128)(2,1)S(1)}, bf16[768,256]{1,0:T(8,128)(2,1)S(1)}, u32[]{:S(2)}, u32[]{:S(2)}) collective-permute-start(bf16[768,256]{1,0:T(8,128)(2,1)S(1)} %pad_maximum_fusion.2), channel_id=1, source_target_pairs={{0,8},{1,33},{2,10},{3,35},{4,12},{5,37},{6,14},{7,39},{8,0},{9,41... | collective-permute-start | bytes 1179656 | tf_op jit(solution)/shard_map/ppermute | solution.py:32
  41.7 14.2 %collective-permute-start.5 = (bf16[2,768,256]{2,1,0:T(8,128)(2,1)S(1)}, bf16[2,768,256]{2,1,0:T(8,128)(2,1)S(1)}, u32[]{:S(2)}, u32[]{:S(2)}) collective-permute-start(bf16[2,768,256]{2,1,0:T(8,128)(2,1)S(1)} %pad_maximum_fusion.1.refs_3_.refs_1_), channel_id=1, source_target_pairs={{0,96},{1,25},{2,98},{3,27},{4,100},{5,29},{6,102},{7,31},{8,104},... | collective-permute-start | bytes 2359304 | tf_op jit(solution)/shard_map/ppermute | solution.py:32
  44.2 13.7 %collective-permute-start.4 = (bf16[2,768,256]{2,1,0:T(8,128)(2,1)S(1)}, bf16[2,768,256]{2,1,0:T(8,128)(2,1)S(1)}, u32[]{:S(2)}, u32[]{:S(2)}) collective-permute-start(bf16[2,768,256]{2,1,0:T(8,128)(2,1)S(1)} %pad_maximum_fusion.refs_2_.refs_0_), channel_id=1, source_target_pairs={{0,32},{1,9},{2,34},{3,11},{4,36},{5,13},{6,38},{7,15},{8,40},{9,1... | collective-permute-start | bytes 2359304 | tf_op jit(solution)/shard_map/ppermute | solution.py:32
  46.1 19.6 %collective-permute-start.6 = (bf16[2,768,256]{2,1,0:T(8,128)(2,1)S(1)}, bf16[2,768,256]{2,1,0:T(8,128)(2,1)}, u32[]{:S(2)}, u32[]{:S(2)}) collective-permute-start(bf16[2,768,256]{2,1,0:T(8,128)(2,1)S(1)} %pad_maximum_fusion.1.refs_3_.refs_1_), channel_id=1, source_target_pairs={{0,32},{1,9},{2,34},{3,11},{4,36},{5,13},{6,38},{7,15},{8,40},{9,1... | collective-permute-start | bytes 2359304 | tf_op jit(solution)/shard_map/ppermute | solution.py:32
  49.5 16.3 %collective-permute-start.7 = (bf16[2,768,256]{2,1,0:T(8,128)(2,1)S(1)}, bf16[2,768,256]{2,1,0:T(8,128)(2,1)}, u32[]{:S(2)}, u32[]{:S(2)}) collective-permute-start(bf16[2,768,256]{2,1,0:T(8,128)(2,1)S(1)} %pad_maximum_fusion.refs_2_.refs_0_), channel_id=1, source_target_pairs={{0,96},{1,25},{2,98},{3,27},{4,100},{5,29},{6,102},{7,31},{8,104},... | collective-permute-start | bytes 2359304 | tf_op jit(solution)/shard_map/ppermute | solution.py:32
  55.9 27.6 %collective-permute-start.8 = (bf16[2,768,256]{2,1,0:T(8,128)(2,1)S(1)}, bf16[2,768,256]{2,1,0:T(8,128)(2,1)S(1)}, u32[]{:S(2)}, u32[]{:S(2)}) collective-permute-start(bf16[2,768,256]{2,1,0:T(8,128)(2,1)S(1)} %collective-permute-done.5.refs_5_.refs_3_), channel_id=1, source_target_pairs={{0,32},{1,9},{2,34},{3,11},{4,36},{5,13},{6,38},{7,15},{8,40},{9,1... | collective-permute-start | bytes 2359304 | tf_op jit(solution)/shard_map/ppermute | solution.py:32
  57.9 25.7 %collective-permute-start.9 = (bf16[2,768,256]{2,1,0:T(8,128)(2,1)S(1)}, bf16[2,768,256]{2,1,0:T(8,128)(2,1)S(1)}, u32[]{:S(2)}, u32[]{:S(2)}) collective-permute-start(bf16[2,768,256]{2,1,0:T(8,128)(2,1)S(1)} %collective-permute-done.4.refs_4_.refs_2_), channel_id=1, source_target_pairs={{0,96},{1,25},{2,98},{3,27},{4,100},{5,29},{6,102},{7,31},{8,104},... | collective-permute-start | bytes 2359304 | tf_op jit(solution)/shard_map/ppermute | solution.py:32
  65.8 1.6 %copy-start = (bf16[128,8192]{1,0:T(8,128)(2,1)S(1)}, bf16[128,8192]{1,0:T(8,128)(2,1)}, u32[]{:S(2)}) copy-start(bf16[128,8192]{1,0:T(8,128)(2,1)} %refs_0_.1) | copy-start | bytes 6291460
  67.4 9.0 %copy-start.1 = (f32[1,3,64,256]{3,2,1,0:T(8,128)S(1)}, f32[1,3,64,256]{3,2,1,0:T(8,128)}, u32[]{:S(2)}) copy-start(f32[1,3,64,256]{3,2,1,0:T(8,128)} %param.11) | copy-start | bytes 589828
  72.3 35.6 %collective-permute-start.10 = (bf16[6,2,256,256]{3,2,1,0:T(8,128)(2,1)S(1)}, bf16[6,2,256,256]{3,2,1,0:T(8,128)(2,1)S(1)}, u32[]{:S(2)}, u32[]{:S(2)}) collective-permute-start(bf16[6,2,256,256]{3,2,1,0:T(8,128)(2,1)S(1)} %get-tuple-element.13), channel_id=1, source_target_pairs={{0,1},{1,0},{2,3},{3,2},{4,5},{5,4},{6,7},{7,6},{8,9},{9,8},{10,11... | collective-permute-start | bytes 4718600 | tf_op jit(solution)/shard_map/ppermute | solution.py:32
  76.4 16.7 %collective-permute-start.12 = (bf16[3,64,256]{2,1,0:T(8,128)(2,1)S(1)}, bf16[3,64,256]{2,1,0:T(8,128)(2,1)S(1)}, u32[]{:S(2)}, u32[]{:S(2)}) collective-permute-start(bf16[3,64,256]{2,1,0:T(8,128)(2,1)S(1)} %convert_element_type.18), channel_id=1, source_target_pairs={{0,128},{1,129},{2,130},{3,131},{4,132},{5,133},{6,134},{7,135},{8... | collective-permute-start | bytes 294920 | tf_op jit(solution)/shard_map/ppermute | solution.py:32
  84.1 23.8 %collective-permute-start.11 = (bf16[1152,256]{1,0:T(8,128)(2,1)S(1)}, bf16[1152,256]{1,0:T(8,128)(2,1)S(1)}, u32[]{:S(2)}, u32[]{:S(2)}) collective-permute-start(bf16[1152,256]{1,0:T(8,128)(2,1)S(1)} %get-tuple-element.14), channel_id=1, source_target_pairs={{0,1},{1,0},{2,3},{3,2},{4,5},{5,4},{6,7},{7,6},{8,9},{9,8},{10,11... | collective-permute-start | bytes 1769480 | tf_op jit(solution)/shard_map/ppermute | solution.py:32
  93.2 14.0 %collective-permute-start.13 = (bf16[3,64,256]{2,1,0:T(8,128)(2,1)S(1)}, bf16[3,64,256]{2,1,0:T(8,128)(2,1)S(1)}, u32[]{:S(2)}, u32[]{:S(2)}) collective-permute-start(bf16[3,64,256]{2,1,0:T(8,128)(2,1)S(1)} %add_convert_fusion), channel_id=1, source_target_pairs={{0,384},{1,385},{2,386},{3,387},{4,388},{5,389},{6,390},{7,391},{8... | collective-permute-start | bytes 294920 | tf_op jit(solution)/shard_map/ppermute | solution.py:32

commit v2 on v1

--- a/solution.py
+++ b/solution.py
@@ -121,20 +121,27 @@
 
 def early_kernel(at_ref, *refs):
     n = len(EARLY)
-    toks, pieces = refs[:2], refs[2 : 2 + n]
-    out_ref, down_ref, late_tok_ref, tok_ref, sems, late_sems = refs[2 + n :]
+    toks, pieces = refs[:2], list(refs[2 : 2 + n])
+    out_ref, down_ref, late_tok_ref, tok_ref, held, sems, late_sems, held_sems = refs[2 + n :]
+    loads = {}
+    for i in range(held.shape[0]):
+        s = n - held.shape[0] + i
+        loads[s] = pltpu.make_async_copy(pieces[s], held.at[i], held_sems.at[i])
+        pieces[s] = held.at[i]
     copies = token_copies(EARLY, at_ref, toks, tok_ref, sems)
     late_copies = token_copies(LATE, at_ref, toks, late_tok_ref, late_sems)
-    for copy in copies + late_copies:
+    for copy in copies[:8] + list(loads.values()) + copies[8:] + late_copies:
         copy.start()
-    for s in range(n):
-        down_ref[s] = pieces[s][:, SHARE:, :]
     total = jnp.zeros((2 * toks[0].shape[0], WIDE), jnp.float32)
     square = jnp.zeros((2 * toks[0].shape[0], LANES), jnp.float32)
-    for s, i in itertools.product(range(n), range(2)):
-        for who in range(2):
-            copies[4 * s + 2 * i + who].wait()
-        total, square = add_piece(total, square, tok_ref[s, i], pieces[s][i, :SHARE, :])
+    for s in range(n):
+        if s in loads:
+            loads[s].wait()
+        down_ref[s] = pieces[s][:, SHARE:, :]
+        for i in range(2):
+            for who in range(2):
+                copies[4 * s + 2 * i + who].wait()
+            total, square = add_piece(total, square, tok_ref[s, i], pieces[s][i, :SHARE, :])
     out_ref[:, :WIDE] = total
     out_ref[:, WIDE:] = square
     for copy in late_copies:
@@ -143,8 +150,8 @@
 
 def late_kernel(before_ref, tok_ref, *refs):
     n = len(LATE)
-    pieces, (mine_ref, send_ref) = refs[:n], refs[n:]
-    rows = mine_ref.shape[0]
+    pieces, send_ref = refs[:n], refs[n]
+    rows = tok_ref.shape[2] // 2
     for part, (s, i) in enumerate(itertools.product(range(n), range(2))):
         send_ref[part * HALF : (part + 1) * HALF, :] = pieces[s][i, SHARE:, :]
     total, square = before_ref[:, :WIDE], before_ref[:, WIDE:]
@@ -154,7 +161,6 @@
     total = total * lax.rsqrt(mean + EPS)
     gate, up = total[:, : WIDE // 2], total[:, WIDE // 2 :]
     hidden = (gate / (1.0 + jnp.exp(-gate)) * up).astype(jnp.bfloat16)
-    mine_ref[...] = hidden[:rows]
     send_ref[2 * n * HALF :, : WIDE // 2] = hidden[rows:]
     send_ref[2 * n * HALF :, WIDE // 2 :] = hidden[:rows]
 
@@ -175,12 +181,14 @@
             jax.ShapeDtypeStruct((n, 2, HALF, WIDE), jnp.bfloat16),
             jax.ShapeDtypeStruct((m, 2, 2 * rows, SHARE), jnp.bfloat16),
         ],
-        in_specs=[SMEM] + [HBM] * 2 + [VMEM] * n,
+        in_specs=[SMEM] + [HBM] * 2 + [VMEM] * (n - 2) + [HBM] * 2,
         out_specs=[VMEM, VMEM, VMEM],
         scratch_shapes=[
             pltpu.VMEM((n, 2, 2 * rows, SHARE), jnp.bfloat16),
+            pltpu.VMEM((2, 2, SHARE + HALF, WIDE), jnp.bfloat16),
             pltpu.SemaphoreType.DMA((n, 2, 2)),
             pltpu.SemaphoreType.DMA((m, 2, 2)),
+            pltpu.SemaphoreType.DMA((2,)),
         ],
         name="early",
         **sums_params(n),
@@ -191,63 +199,55 @@
     n = len(LATE)
     return pl.pallas_call(
         late_kernel,
-        out_shape=[
-            jax.ShapeDtypeStruct((rows, WIDE // 2), jnp.bfloat16),
-            jax.ShapeDtypeStruct((2 * n * HALF + rows, WIDE), jnp.bfloat16),
-        ],
+        out_shape=jax.ShapeDtypeStruct((2 * n * HALF + rows, WIDE), jnp.bfloat16),
         in_specs=[VMEM] * (2 + n),
-        out_specs=[VMEM, VMEM],
+        out_specs=VMEM,
         name="late",
         **sums_params(n),
     )(before, late_tokens, *[pieces[s] for s in LATE])
 
 
-def down_kernel(at_ref, mine_ref, early_ref, late_ref, *refs):
-    n = len(ORDER)
-    own, (out_ref, out_held, out_sems) = refs[:n], refs[n:]
-    mine, theirs = mine_ref[...], late_ref[2 * len(LATE) * HALF :, : WIDE // 2]
+def down_kernel(at_ref, own_early_ref, own_late_ref, early_ref, late_ref, out_ref, held, sems):
+    half = WIDE // 2
+    hid = 2 * len(LATE) * HALF
+    mine, theirs = own_late_ref[hid:, half:], late_ref[hid:, :half]
     hidden = jnp.where(
         at_ref[48] == 0,
         jnp.concatenate([mine, theirs], axis=1),
         jnp.concatenate([theirs, mine], axis=1),
     )
     copies = []
-    for slot, (s, i, who) in enumerate(itertools.product(range(n), range(2), range(2))):
-        a, half = ORDER[s]
-        if who == 0:
-            rows = own[s][i, SHARE:, :]
-        elif s < len(EARLY):
-            rows = early_ref[s, i]
+    for slot, (s, i, who) in enumerate(itertools.product(range(len(ORDER)), range(2), range(2))):
+        a, which = ORDER[s]
+        if s < len(EARLY):
+            rows = (own_early_ref, early_ref)[who][s, i]
         else:
             part = 2 * (s - len(EARLY)) + i
-            rows = late_ref[part * HALF : (part + 1) * HALF, :]
+            rows = (own_late_ref, late_ref)[who][part * HALF : (part + 1) * HALF, :]
         out = lax.dot_general(hidden, rows, ROW_DIMS, preferred_element_type=jnp.float32)
-        out_held[slot] = out.astype(out_held.dtype)
-        start = pl.multiple_of(at_ref[16 + 16 * who + 4 * a + HALVES[half][i]], HALF)
-        copy = pltpu.make_async_copy(
-            out_held.at[slot], out_ref.at[:, pl.ds(start, HALF)], out_sems.at[slot]
-        )
+        held[slot] = out.astype(held.dtype)
+        start = pl.multiple_of(at_ref[16 + 16 * who + 4 * a + HALVES[which][i]], HALF)
+        copy = pltpu.make_async_copy(held.at[slot], out_ref.at[:, pl.ds(start, HALF)], sems.at[slot])
         copy.start()
         copies.append(copy)
     for copy in copies:
         copy.wait()
 
 
-def down(at, mine, early, late, own, tokens):
+def down(at, own_early, own_late, early, late, tokens):
     n = len(ORDER)
-    rows = tokens.shape[0]
     return pl.pallas_call(
         down_kernel,
         out_shape=jax.ShapeDtypeStruct(tokens.shape, jnp.bfloat16),
-        in_specs=[SMEM] + [VMEM] * (n + 3),
+        in_specs=[SMEM] + [VMEM] * 4,
         out_specs=HBM,
         scratch_shapes=[
-            pltpu.VMEM((4 * n, rows, HALF), jnp.bfloat16),
+            pltpu.VMEM((4 * n, tokens.shape[0], HALF), jnp.bfloat16),
             pltpu.SemaphoreType.DMA((4 * n,)),
         ],
         compiler_params=pltpu.CompilerParams(vmem_limit_bytes=8 * 2**20),
         name="down",
-    )(at, mine, early, late, *[own[s] for s in ORDER])
+    )(at, own_early, own_late, early, late)
 
 
 def per_device(sizes, tokens, norm_gain, gate_weight, up_weight, down_weight, slice_grads):
@@ -289,14 +289,14 @@
         ]
     ).astype(jnp.int32)
 
-    total, early, late_tokens = early_sums(at, both_tokens, own)
-    early = move(early, other_core)
+    total, own_early, late_tokens = early_sums(at, both_tokens, own)
+    early = move(own_early, other_core)
     pair = (mine.astype(jnp.float32) + far.astype(jnp.float32)).astype(jnp.bfloat16)
     rest = move(pair, over_cuts(3))
     grad_mean = (pair.astype(jnp.float32) + rest.astype(jnp.float32)) / sizes[0]
-    mine_hidden, late = late_sums(total, late_tokens, tokens.shape[0], own)
-    late = move(late, other_core)
-    branch = down(at, mine_hidden, early, late, own, tokens)
+    own_late = late_sums(total, late_tokens, tokens.shape[0], own)
+    late = move(own_late, other_core)
+    branch = down(at, own_early, own_late, early, late, tokens)
     return branch, grad_mean
 
 

time: 112 us -> 111 us (level)
  Pallas kernels: 10.9 us -> 9.26 us
where the time goes in v2:
time: 111 us; the launch traced here: 110 us
  starting transfers between devices  54.6 us (49%)
  waiting for transfers between devices  26.5 us (24%)
  blocking collectives  16.3 us (15%)
  Pallas kernels  9.26 us (8%)
  local copies, waits for them, and re-layouts  1.63 us (1%)
    ppermute x14, starting transfers between devices, moved(): return lax.ppermute(value, AXES, pairs)  54.6 us
    ppermute x14, waiting for transfers between devices, moved(): return lax.ppermute(value, AXES, pairs)  26.5 us
    all_gather x1, blocking collectives, per_device(): near = lax.all_gather(packed, ('z', 'k'), axis=0, tiled=True)  16.3 us
    pallas_call x1, Pallas kernels, early_sums(): pl.pallas_call(early_kernel, out_shape=[jax.ShapeDtypeStruct((2 * rows, W...  4.19 us
    pallas_call x1, Pallas kernels, down(): pl.pallas_call(down_kernel, out_shape=jax.ShapeDtypeStruct(tokens.shape,...  2.99 us
  transfers between devices with their start and end apart: 14, of which 6 were waited for; matrix products, arithmetic and copies ran while one was open for 1% of the time, Pallas kernels for 6%

profile of v2, /device:TPU:1, one launch (start us, length us, event | category | flops | bytes accessed | tf_op | source)
XLA Modules:
  0.0 110.1 jit_solution(14929494269000246152)
XLA Ops:
  0.6 8.8 %collective-permute-start = (bf16[128,8192]{1,0:T(8,128)(2,1)}, bf16[128,8192]{1,0:T(8,128)(2,1)}, u32[]{:S(2)}, u32[]{:S(2)}) collective-permute-start(bf16[128,8192]{1,0:T(8,128)(2,1)} %refs_0_.1), channel_id=1, source_target_pairs={{0,1},{1,0},{2,3},{3,2},{4,5},{5,4},{6,7},{7,6},{8,9},{9,8},{10,11... | collective-permute-start | bytes 6291464 | tf_op jit(solution)/shard_map/ppermute | solution.py:32
  9.4 1.6 %pack.1 = bf16[64,768]{1,0:T(8,128)(2,1)} custom-call(bf16[1,64]{1,0:T(2,128)(2,1)} %bitcast.15, bf16[64,256]{1,0:T(8,128)(2,1)} %gate_hbm.1, bf16[64,256]{1,0:T(8,128)(2,1)} %up_hbm.1, bf16[64,256]{1,0:T(8,128)(2,1)} %bitcast.14), custom_call_target="tpu_custom_call" | custom-call | tf_op jit(solution)/shard_map/pack/pallas_call | solution.py:82
  11.0 16.3 %all_gather.3 = bf16[512,768]{1,0:T(8,128)(2,1)S(1)} all-gather(bf16[64,768]{1,0:T(8,128)(2,1)} %pack.1), channel_id=1, replica_groups=mesh['c'=4,'y'=4,'x'=4,'z'=4,'k'=2] {'z','k'}, dimensions={0}, use_global_device_ids=true | all-gather | bytes 884736 | tf_op jit(solution)/shard_map/all_gather | solution.py:257
  27.4 1.9 %collective-permute-start.2 = (bf16[768,256]{1,0:T(8,128)(2,1)S(1)}, bf16[768,256]{1,0:T(8,128)(2,1)S(1)}, u32[]{:S(2)}, u32[]{:S(2)}) collective-permute-start(bf16[768,256]{1,0:T(8,128)(2,1)S(1)} %pad_maximum_fusion.2), channel_id=1, source_target_pairs={{0,24},{1,97},{2,26},{3,99},{4,28},{5,101},{6,30},{7,103},{8,16},{... | collective-permute-start | bytes 1179656 | tf_op jit(solution)/shard_map/ppermute | solution.py:32
  29.3 1.9 %collective-permute-start.3 = (bf16[768,256]{1,0:T(8,128)(2,1)S(1)}, bf16[768,256]{1,0:T(8,128)(2,1)S(1)}, u32[]{:S(2)}, u32[]{:S(2)}) collective-permute-start(bf16[768,256]{1,0:T(8,128)(2,1)S(1)} %pad_maximum_fusion.2), channel_id=1, source_target_pairs={{0,16},{1,65},{2,18},{3,67},{4,20},{5,69},{6,22},{7,71},{8,24},{9,... | collective-permute-start | bytes 1179656 | tf_op jit(solution)/shard_map/ppermute | solution.py:32
  31.2 5.1 %collective-permute-start.1 = (bf16[768,256]{1,0:T(8,128)(2,1)S(1)}, bf16[768,256]{1,0:T(8,128)(2,1)S(1)}, u32[]{:S(2)}, u32[]{:S(2)}) collective-permute-start(bf16[768,256]{1,0:T(8,128)(2,1)S(1)} %pad_maximum_fusion.2), channel_id=1, source_target_pairs={{0,8},{1,33},{2,10},{3,35},{4,12},{5,37},{6,14},{7,39},{8,0},{9,41... | collective-permute-start | bytes 1179656 | tf_op jit(solution)/shard_map/ppermute | solution.py:32
  36.4 5.2 %collective-permute-done.2 = bf16[768,256]{1,0:T(8,128)(2,1)S(1)} collective-permute-done((bf16[768,256]{1,0:T(8,128)(2,1)S(1)}, bf16[768,256]{1,0:T(8,128)(2,1)S(1)}, u32[]{:S(2)}, u32[]{:S(2)}) %collective-permute-start.2) | collective-permute-done | bytes 393248 | tf_op jit(solution)/shard_map/ppermute | solution.py:32
  41.6 0.0 collective-permute-done.3
  41.6 0.1 pad_maximum_fusion.1.refs_3_
  41.7 1.9 %collective-permute-start.5 = (bf16[2,768,256]{2,1,0:T(8,128)(2,1)S(1)}, bf16[2,768,256]{2,1,0:T(8,128)(2,1)S(1)}, u32[]{:S(2)}, u32[]{:S(2)}) collective-permute-start(bf16[2,768,256]{2,1,0:T(8,128)(2,1)S(1)} %pad_maximum_fusion.1.refs_3_), channel_id=1, source_target_pairs={{0,96},{1,25},{2,98},{3,27},{4,100},{5,29},{6,102},{7,31},{8,104},... | collective-permute-start | bytes 2359304 | tf_op jit(solution)/shard_map/ppermute | solution.py:32
  43.6 0.5 collective-permute-done.1
  44.1 0.1 pad_maximum_fusion.refs_2_
  44.2 1.9 %collective-permute-start.4 = (bf16[2,768,256]{2,1,0:T(8,128)(2,1)S(1)}, bf16[2,768,256]{2,1,0:T(8,128)(2,1)S(1)}, u32[]{:S(2)}, u32[]{:S(2)}) collective-permute-start(bf16[2,768,256]{2,1,0:T(8,128)(2,1)S(1)} %pad_maximum_fusion.refs_2_), channel_id=1, source_target_pairs={{0,32},{1,9},{2,34},{3,11},{4,36},{5,13},{6,38},{7,15},{8,40},{9,1... | collective-permute-start | bytes 2359304 | tf_op jit(solution)/shard_map/ppermute | solution.py:32
  46.1 3.4 %collective-permute-start.6 = (bf16[2,768,256]{2,1,0:T(8,128)(2,1)S(1)}, bf16[2,768,256]{2,1,0:T(8,128)(2,1)}, u32[]{:S(2)}, u32[]{:S(2)}) collective-permute-start(bf16[2,768,256]{2,1,0:T(8,128)(2,1)S(1)} %pad_maximum_fusion.1.refs_3_), channel_id=1, source_target_pairs={{0,32},{1,9},{2,34},{3,11},{4,36},{5,13},{6,38},{7,15},{8,40},{9,1... | collective-permute-start | bytes 2359304 | tf_op jit(solution)/shard_map/ppermute | solution.py:32
  49.5 4.1 %collective-permute-start.7 = (bf16[2,768,256]{2,1,0:T(8,128)(2,1)S(1)}, bf16[2,768,256]{2,1,0:T(8,128)(2,1)}, u32[]{:S(2)}, u32[]{:S(2)}) collective-permute-start(bf16[2,768,256]{2,1,0:T(8,128)(2,1)S(1)} %pad_maximum_fusion.refs_2_), channel_id=1, source_target_pairs={{0,96},{1,25},{2,98},{3,27},{4,100},{5,29},{6,102},{7,31},{8,104},... | collective-permute-start | bytes 2359304 | tf_op jit(solution)/shard_map/ppermute | solution.py:32
  53.6 0.1 pad_add_fusion.at_ref
  53.7 2.2 %collective-permute-done.5.refs_5_ = bf16[2,768,256]{2,1,0:T(8,128)(2,1)S(1)} collective-permute-done((bf16[2,768,256]{2,1,0:T(8,128)(2,1)S(1)}, bf16[2,768,256]{2,1,0:T(8,128)(2,1)S(1)}, u32[]{:S(2)}, u32[]{:S(2)}) %collective-permute-start.5) | collective-permute-done | bytes 786464 | tf_op jit(solution)/shard_map/ppermute | solution.py:32
  55.9 1.9 %collective-permute-start.8 = (bf16[2,768,256]{2,1,0:T(8,128)(2,1)S(1)}, bf16[2,768,256]{2,1,0:T(8,128)(2,1)S(1)}, u32[]{:S(2)}, u32[]{:S(2)}) collective-permute-start(bf16[2,768,256]{2,1,0:T(8,128)(2,1)S(1)} %collective-permute-done.5.refs_5_), channel_id=1, source_target_pairs={{0,32},{1,9},{2,34},{3,11},{4,36},{5,13},{6,38},{7,15},{8,40},{9,1... | collective-permute-start | bytes 2359304 | tf_op jit(solution)/shard_map/ppermute | solution.py:32
  57.9 0.0 collective-permute-done.4.refs_4_
  57.9 3.6 %collective-permute-start.9 = (bf16[2,768,256]{2,1,0:T(8,128)(2,1)S(1)}, bf16[2,768,256]{2,1,0:T(8,128)(2,1)S(1)}, u32[]{:S(2)}, u32[]{:S(2)}) collective-permute-start(bf16[2,768,256]{2,1,0:T(8,128)(2,1)S(1)} %collective-permute-done.4.refs_4_), channel_id=1, source_target_pairs={{0,96},{1,25},{2,98},{3,27},{4,100},{5,29},{6,102},{7,31},{8,104},... | collective-permute-start | bytes 2359304 | tf_op jit(solution)/shard_map/ppermute | solution.py:32
  61.4 4.3 %collective-permute-done.6.refs_6_ = bf16[2,768,256]{2,1,0:T(8,128)(2,1)} collective-permute-done((bf16[2,768,256]{2,1,0:T(8,128)(2,1)S(1)}, bf16[2,768,256]{2,1,0:T(8,128)(2,1)}, u32[]{:S(2)}, u32[]{:S(2)}) %collective-permute-start.6) | collective-permute-done | bytes 786464 | tf_op jit(solution)/shard_map/ppermute | solution.py:32
  65.8 0.0 collective-permute-done.7.refs_7_
  65.8 0.0 collective-permute-done.refs_1_
  65.8 0.0 copy-start
  65.8 1.6 %copy-done = bf16[128,8192]{1,0:T(8,128)(2,1)S(1)} copy-done((bf16[128,8192]{1,0:T(8,128)(2,1)S(1)}, bf16[128,8192]{1,0:T(8,128)(2,1)}, u32[]{:S(2)}) %copy-start) | copy-done | bytes 2097176
  67.4 0.0 copy-start.1
  67.4 4.2 %early.1 = (f32[256,384]{1,0:T(8,128)S(1)}, bf16[6,2,256,256]{3,2,1,0:T(8,128)(2,1)S(1)}, bf16[2,2,256,512]{3,2,1,0:T(8,128)(2,1)S(1)}) custom-call(s32[49]{0:T(128)S(1)} %pad_add_fusion.at_ref, bf16[128,8192]{1,0:T(8,128)(2,1)S(1)} %copy-done, bf16[128,8192]{1,0:T(8,128)(2,1)} %collective-permute-done.refs_1_, ...), custom_call_target="tpu_custom_call" | custom-call | flops 6442450944 | bytes 6291456 | tf_op jit(solution)/shard_map/early/pallas_call | solution.py:177
  71.6 4.1 %collective-permute-start.10 = (bf16[6,2,256,256]{3,2,1,0:T(8,128)(2,1)S(1)}, bf16[6,2,256,256]{3,2,1,0:T(8,128)(2,1)S(1)}, u32[]{:S(2)}, u32[]{:S(2)}) collective-permute-start(bf16[6,2,256,256]{3,2,1,0:T(8,128)(2,1)S(1)} %get-tuple-element.8.own_early_ref), channel_id=1, source_target_pairs={{0,1},{1,0},{2,3},{3,2},{4,5},{5,4},{6,7},{7,6},{8,9},{9,8},{10,11... | collective-permute-start | bytes 4718600 | tf_op jit(solution)/shard_map/ppermute | solution.py:32
  75.6 0.0 copy-done.1
  75.7 7.1 %collective-permute-start.12 = (bf16[3,64,256]{2,1,0:T(8,128)(2,1)S(1)}, bf16[3,64,256]{2,1,0:T(8,128)(2,1)S(1)}, u32[]{:S(2)}, u32[]{:S(2)}) collective-permute-start(bf16[3,64,256]{2,1,0:T(8,128)(2,1)S(1)} %convert_element_type.18), channel_id=1, source_target_pairs={{0,128},{1,129},{2,130},{3,131},{4,132},{5,133},{6,134},{7,135},{8... | collective-permute-start | bytes 294920 | tf_op jit(solution)/shard_map/ppermute | solution.py:32
  82.8 0.0 collective-permute-done.8.refs_0_
  82.8 0.0 collective-permute-done.9.refs_1_
  82.8 0.5 late.1.own_late_ref
  83.3 2.2 %collective-permute-start.11 = (bf16[1152,256]{1,0:T(8,128)(2,1)S(1)}, bf16[1152,256]{1,0:T(8,128)(2,1)S(1)}, u32[]{:S(2)}, u32[]{:S(2)}) collective-permute-start(bf16[1152,256]{1,0:T(8,128)(2,1)S(1)} %late.1.own_late_ref), channel_id=1, source_target_pairs={{0,1},{1,0},{2,3},{3,2},{4,5},{5,4},{6,7},{7,6},{8,9},{9,8},{10,11... | collective-permute-start | bytes 1769480 | tf_op jit(solution)/shard_map/ppermute | solution.py:32
  85.5 6.8 %collective-permute-done.12 = bf16[3,64,256]{2,1,0:T(8,128)(2,1)S(1)} collective-permute-done((bf16[3,64,256]{2,1,0:T(8,128)(2,1)S(1)}, bf16[3,64,256]{2,1,0:T(8,128)(2,1)S(1)}, u32[]{:S(2)}, u32[]{:S(2)}) %collective-permute-start.12) | collective-permute-done | bytes 98336 | tf_op jit(solution)/shard_map/ppermute | solution.py:32
  92.4 6.7 %collective-permute-start.13 = (bf16[3,64,256]{2,1,0:T(8,128)(2,1)S(1)}, bf16[3,64,256]{2,1,0:T(8,128)(2,1)S(1)}, u32[]{:S(2)}, u32[]{:S(2)}) collective-permute-start(bf16[3,64,256]{2,1,0:T(8,128)(2,1)S(1)} %add_convert_fusion), channel_id=1, source_target_pairs={{0,384},{1,385},{2,386},{3,387},{4,388},{5,389},{6,390},{7,391},{8... | collective-permute-start | bytes 294920 | tf_op jit(solution)/shard_map/ppermute | solution.py:32
  99.1 7.3 %collective-permute-done.13 = bf16[3,64,256]{2,1,0:T(8,128)(2,1)S(1)} collective-permute-done((bf16[3,64,256]{2,1,0:T(8,128)(2,1)S(1)}, bf16[3,64,256]{2,1,0:T(8,128)(2,1)S(1)}, u32[]{:S(2)}, u32[]{:S(2)}) %collective-permute-start.13) | collective-permute-done | bytes 98336 | tf_op jit(solution)/shard_map/ppermute | solution.py:32
  106.4 0.7 add_multiply_fusion
  107.1 0.0 collective-permute-done.11.late_ref
  107.1 0.0 collective-permute-done.10.early_ref
  107.1 3.0 %down.1 = bf16[128,8192]{1,0:T(8,128)(2,1)} custom-call(s32[49]{0:T(128)S(1)} %pad_add_fusion.at_ref, bf16[6,2,256,256]{3,2,1,0:T(8,128)(2,1)S(1)} %get-tuple-element.8.own_early_ref, bf16[1152,256]{1,0:T(8,128)(2,1)S(1)} %late.1.own_late_ref, bf16[6,2,256,256]{3,2,1,0:T(8,128)(2,1)S(1)} %collective-permute-done.10.early_ref, ...), custom_call_target="tpu_custom_call" | custom-call | tf_op jit(solution)/shard_map/down/pallas_call | solution.py:239
  (7 shorter events, 0.1 us)
Async XLA Ops:
  0.6 65.1 %collective-permute-start = (bf16[128,8192]{1,0:T(8,128)(2,1)}, bf16[128,8192]{1,0:T(8,128)(2,1)}, u32[]{:S(2)}, u32[]{:S(2)}) collective-permute-start(bf16[128,8192]{1,0:T(8,128)(2,1)} %refs_0_.1), channel_id=1, source_target_pairs={{0,1},{1,0},{2,3},{3,2},{4,5},{5,4},{6,7},{7,6},{8,9},{9,8},{10,11... | collective-permute-start | bytes 6291464 | tf_op jit(solution)/shard_map/ppermute | solution.py:32
  27.4 14.2 %collective-permute-start.2 = (bf16[768,256]{1,0:T(8,128)(2,1)S(1)}, bf16[768,256]{1,0:T(8,128)(2,1)S(1)}, u32[]{:S(2)}, u32[]{:S(2)}) collective-permute-start(bf16[768,256]{1,0:T(8,128)(2,1)S(1)} %pad_maximum_fusion.2), channel_id=1, source_target_pairs={{0,24},{1,97},{2,26},{3,99},{4,28},{5,101},{6,30},{7,103},{8,16},{... | collective-permute-start | bytes 1179656 | tf_op jit(solution)/shard_map/ppermute | solution.py:32
  29.3 12.3 %collective-permute-start.3 = (bf16[768,256]{1,0:T(8,128)(2,1)S(1)}, bf16[768,256]{1,0:T(8,128)(2,1)S(1)}, u32[]{:S(2)}, u32[]{:S(2)}) collective-permute-start(bf16[768,256]{1,0:T(8,128)(2,1)S(1)} %pad_maximum_fusion.2), channel_id=1, source_target_pairs={{0,16},{1,65},{2,18},{3,67},{4,20},{5,69},{6,22},{7,71},{8,24},{9,... | collective-permute-start | bytes 1179656 | tf_op jit(solution)/shard_map/ppermute | solution.py:32
  31.2 12.9 %collective-permute-start.1 = (bf16[768,256]{1,0:T(8,128)(2,1)S(1)}, bf16[768,256]{1,0:T(8,128)(2,1)S(1)}, u32[]{:S(2)}, u32[]{:S(2)}) collective-permute-start(bf16[768,256]{1,0:T(8,128)(2,1)S(1)} %pad_maximum_fusion.2), channel_id=1, source_target_pairs={{0,8},{1,33},{2,10},{3,35},{4,12},{5,37},{6,14},{7,39},{8,0},{9,41... | collective-permute-start | bytes 1179656 | tf_op jit(solution)/shard_map/ppermute | solution.py:32
  41.7 14.2 %collective-permute-start.5 = (bf16[2,768,256]{2,1,0:T(8,128)(2,1)S(1)}, bf16[2,768,256]{2,1,0:T(8,128)(2,1)S(1)}, u32[]{:S(2)}, u32[]{:S(2)}) collective-permute-start(bf16[2,768,256]{2,1,0:T(8,128)(2,1)S(1)} %pad_maximum_fusion.1.refs_3_), channel_id=1, source_target_pairs={{0,96},{1,25},{2,98},{3,27},{4,100},{5,29},{6,102},{7,31},{8,104},... | collective-permute-start | bytes 2359304 | tf_op jit(solution)/shard_map/ppermute | solution.py:32
  44.2 13.7 %collective-permute-start.4 = (bf16[2,768,256]{2,1,0:T(8,128)(2,1)S(1)}, bf16[2,768,256]{2,1,0:T(8,128)(2,1)S(1)}, u32[]{:S(2)}, u32[]{:S(2)}) collective-permute-start(bf16[2,768,256]{2,1,0:T(8,128)(2,1)S(1)} %pad_maximum_fusion.refs_2_), channel_id=1, source_target_pairs={{0,32},{1,9},{2,34},{3,11},{4,36},{5,13},{6,38},{7,15},{8,40},{9,1... | collective-permute-start | bytes 2359304 | tf_op jit(solution)/shard_map/ppermute | solution.py:32
  46.1 19.6 %collective-permute-start.6 = (bf16[2,768,256]{2,1,0:T(8,128)(2,1)S(1)}, bf16[2,768,256]{2,1,0:T(8,128)(2,1)}, u32[]{:S(2)}, u32[]{:S(2)}) collective-permute-start(bf16[2,768,256]{2,1,0:T(8,128)(2,1)S(1)} %pad_maximum_fusion.1.refs_3_), channel_id=1, source_target_pairs={{0,32},{1,9},{2,34},{3,11},{4,36},{5,13},{6,38},{7,15},{8,40},{9,1... | collective-permute-start | bytes 2359304 | tf_op jit(solution)/shard_map/ppermute | solution.py:32
  49.5 16.3 %collective-permute-start.7 = (bf16[2,768,256]{2,1,0:T(8,128)(2,1)S(1)}, bf16[2,768,256]{2,1,0:T(8,128)(2,1)}, u32[]{:S(2)}, u32[]{:S(2)}) collective-permute-start(bf16[2,768,256]{2,1,0:T(8,128)(2,1)S(1)} %pad_maximum_fusion.refs_2_), channel_id=1, source_target_pairs={{0,96},{1,25},{2,98},{3,27},{4,100},{5,29},{6,102},{7,31},{8,104},... | collective-permute-start | bytes 2359304 | tf_op jit(solution)/shard_map/ppermute | solution.py:32
  55.9 26.8 %collective-permute-start.8 = (bf16[2,768,256]{2,1,0:T(8,128)(2,1)S(1)}, bf16[2,768,256]{2,1,0:T(8,128)(2,1)S(1)}, u32[]{:S(2)}, u32[]{:S(2)}) collective-permute-start(bf16[2,768,256]{2,1,0:T(8,128)(2,1)S(1)} %collective-permute-done.5.refs_5_), channel_id=1, source_target_pairs={{0,32},{1,9},{2,34},{3,11},{4,36},{5,13},{6,38},{7,15},{8,40},{9,1... | collective-permute-start | bytes 2359304 | tf_op jit(solution)/shard_map/ppermute | solution.py:32
  57.9 24.9 %collective-permute-start.9 = (bf16[2,768,256]{2,1,0:T(8,128)(2,1)S(1)}, bf16[2,768,256]{2,1,0:T(8,128)(2,1)S(1)}, u32[]{:S(2)}, u32[]{:S(2)}) collective-permute-start(bf16[2,768,256]{2,1,0:T(8,128)(2,1)S(1)} %collective-permute-done.4.refs_4_), channel_id=1, source_target_pairs={{0,96},{1,25},{2,98},{3,27},{4,100},{5,29},{6,102},{7,31},{8,104},... | collective-permute-start | bytes 2359304 | tf_op jit(solution)/shard_map/ppermute | solution.py:32
  65.8 1.6 %copy-start = (bf16[128,8192]{1,0:T(8,128)(2,1)S(1)}, bf16[128,8192]{1,0:T(8,128)(2,1)}, u32[]{:S(2)}) copy-start(bf16[128,8192]{1,0:T(8,128)(2,1)} %refs_0_.1) | copy-start | bytes 6291460
  67.4 8.3 %copy-start.1 = (f32[1,3,64,256]{3,2,1,0:T(8,128)S(1)}, f32[1,3,64,256]{3,2,1,0:T(8,128)}, u32[]{:S(2)}) copy-start(f32[1,3,64,256]{3,2,1,0:T(8,128)} %param.11) | copy-start | bytes 589828
  71.6 35.6 %collective-permute-start.10 = (bf16[6,2,256,256]{3,2,1,0:T(8,128)(2,1)S(1)}, bf16[6,2,256,256]{3,2,1,0:T(8,128)(2,1)S(1)}, u32[]{:S(2)}, u32[]{:S(2)}) collective-permute-start(bf16[6,2,256,256]{3,2,1,0:T(8,128)(2,1)S(1)} %get-tuple-element.8.own_early_ref), channel_id=1, source_target_pairs={{0,1},{1,0},{2,3},{3,2},{4,5},{5,4},{6,7},{7,6},{8,9},{9,8},{10,11... | collective-permute-start | bytes 4718600 | tf_op jit(solution)/shard_map/ppermute | solution.py:32
  75.7 16.7 %collective-permute-start.12 = (bf16[3,64,256]{2,1,0:T(8,128)(2,1)S(1)}, bf16[3,64,256]{2,1,0:T(8,128)(2,1)S(1)}, u32[]{:S(2)}, u32[]{:S(2)}) collective-permute-start(bf16[3,64,256]{2,1,0:T(8,128)(2,1)S(1)} %convert_element_type.18), channel_id=1, source_target_pairs={{0,128},{1,129},{2,130},{3,131},{4,132},{5,133},{6,134},{7,135},{8... | collective-permute-start | bytes 294920 | tf_op jit(solution)/shard_map/ppermute | solution.py:32
  83.3 23.8 %collective-permute-start.11 = (bf16[1152,256]{1,0:T(8,128)(2,1)S(1)}, bf16[1152,256]{1,0:T(8,128)(2,1)S(1)}, u32[]{:S(2)}, u32[]{:S(2)}) collective-permute-start(bf16[1152,256]{1,0:T(8,128)(2,1)S(1)} %late.1.own_late_ref), channel_id=1, source_target_pairs={{0,1},{1,0},{2,3},{3,2},{4,5},{5,4},{6,7},{7,6},{8,9},{9,8},{10,11... | collective-permute-start | bytes 1769480 | tf_op jit(solution)/shard_map/ppermute | solution.py:32
  92.4 14.0 %collective-permute-start.13 = (bf16[3,64,256]{2,1,0:T(8,128)(2,1)S(1)}, bf16[3,64,256]{2,1,0:T(8,128)(2,1)S(1)}, u32[]{:S(2)}, u32[]{:S(2)}) collective-permute-start(bf16[3,64,256]{2,1,0:T(8,128)(2,1)S(1)} %add_convert_fusion), channel_id=1, source_target_pairs={{0,384},{1,385},{2,386},{3,387},{4,388},{5,389},{6,390},{7,391},{8... | collective-permute-start | bytes 294920 | tf_op jit(solution)/shard_map/ppermute | solution.py:32

commit v3 on v2

--- a/solution.py
+++ b/solution.py
@@ -216,18 +216,24 @@
         jnp.concatenate([mine, theirs], axis=1),
         jnp.concatenate([theirs, mine], axis=1),
     )
+
+    def rows(who, a, j):
+        half = 0 if j in HALVES[0] else 1
+        s, i = ORDER.index((a, half)), HALVES[half].index(j)
+        if s < len(EARLY):
+            return (own_early_ref, early_ref)[who][s, i]
+        part = 2 * (s - len(EARLY)) + i
+        return (own_late_ref, late_ref)[who][part * HALF : (part + 1) * HALF, :]
+
     copies = []
-    for slot, (s, i, who) in enumerate(itertools.product(range(len(ORDER)), range(2), range(2))):
-        a, which = ORDER[s]
-        if s < len(EARLY):
-            rows = (own_early_ref, early_ref)[who][s, i]
-        else:
-            part = 2 * (s - len(EARLY)) + i
-            rows = (own_late_ref, late_ref)[who][part * HALF : (part + 1) * HALF, :]
-        out = lax.dot_general(hidden, rows, ROW_DIMS, preferred_element_type=jnp.float32)
-        held[slot] = out.astype(held.dtype)
-        start = pl.multiple_of(at_ref[16 + 16 * who + 4 * a + HALVES[which][i]], HALF)
-        copy = pltpu.make_async_copy(held.at[slot], out_ref.at[:, pl.ds(start, HALF)], sems.at[slot])
+    for slot, (a, j) in enumerate(itertools.product(range(4), range(4))):
+        for who, block in enumerate((rows(0, a, j), rows(1, j, a))):
+            out = lax.dot_general(hidden, block, ROW_DIMS, preferred_element_type=jnp.float32)
+            side = at_ref[48] if who == 0 else 1 - at_ref[48]
+            lanes = pl.ds(pl.multiple_of(side * HALF, HALF), HALF)
+            held[slot, :, lanes] = out.astype(held.dtype)
+        start = pl.multiple_of(at_ref[slot], SHARE)
+        copy = pltpu.make_async_copy(held.at[slot], out_ref.at[:, pl.ds(start, SHARE)], sems.at[slot])
         copy.start()
         copies.append(copy)
     for copy in copies:
@@ -242,8 +248,8 @@
         in_specs=[SMEM] + [VMEM] * 4,
         out_specs=HBM,
         scratch_shapes=[
-            pltpu.VMEM((4 * n, tokens.shape[0], HALF), jnp.bfloat16),
-            pltpu.SemaphoreType.DMA((4 * n,)),
+            pltpu.VMEM((2 * n, tokens.shape[0], SHARE), jnp.bfloat16),
+            pltpu.SemaphoreType.DMA((2 * n,)),
         ],
         compiler_params=pltpu.CompilerParams(vmem_limit_bytes=8 * 2**20),
         name="down",

time: 111 us -> 111 us (level)
  no operation moved by 1% of the time
where the time goes in v3:
time: 111 us; the launch traced here: 110 us
  starting transfers between devices  54.6 us (49%)
  waiting for transfers between devices  26.5 us (24%)
  blocking collectives  16.3 us (15%)
  Pallas kernels  9.12 us (8%)
  local copies, waits for them, and re-layouts  1.63 us (1%)
    ppermute x14, starting transfers between devices, moved(): return lax.ppermute(value, AXES, pairs)  54.6 us
    ppermute x14, waiting for transfers between devices, moved(): return lax.ppermute(value, AXES, pairs)  26.5 us
    all_gather x1, blocking collectives, per_device(): near = lax.all_gather(packed, ('z', 'k'), axis=0, tiled=True)  16.3 us
    pallas_call x1, Pallas kernels, early_sums(): pl.pallas_call(early_kernel, out_shape=[jax.ShapeDtypeStruct((2 * rows, W...  4.19 us
    pallas_call x1, Pallas kernels, down(): pl.pallas_call(down_kernel, out_shape=jax.ShapeDtypeStruct(tokens.shape,...  2.85 us
  transfers between devices with their start and end apart: 14, of which 6 were waited for; matrix products, arithmetic and copies ran while one was open for 1% of the time, Pallas kernels for 6%

profile of v3, /device:TPU:1, one launch (start us, length us, event | category | flops | bytes accessed | tf_op | source)
XLA Modules:
  0.0 110.0 jit_solution(10337250124186383530)
XLA Ops:
  0.6 8.8 %collective-permute-start = (bf16[128,8192]{1,0:T(8,128)(2,1)}, bf16[128,8192]{1,0:T(8,128)(2,1)}, u32[]{:S(2)}, u32[]{:S(2)}) collective-permute-start(bf16[128,8192]{1,0:T(8,128)(2,1)} %refs_0_.1), channel_id=1, source_target_pairs={{0,1},{1,0},{2,3},{3,2},{4,5},{5,4},{6,7},{7,6},{8,9},{9,8},{10,11... | collective-permute-start | bytes 6291464 | tf_op jit(solution)/shard_map/ppermute | solution.py:32
  9.4 1.6 %pack.1 = bf16[64,768]{1,0:T(8,128)(2,1)} custom-call(bf16[1,64]{1,0:T(2,128)(2,1)} %bitcast.15, bf16[64,256]{1,0:T(8,128)(2,1)} %gate_hbm.1, bf16[64,256]{1,0:T(8,128)(2,1)} %up_hbm.1, bf16[64,256]{1,0:T(8,128)(2,1)} %bitcast.14), custom_call_target="tpu_custom_call" | custom-call | tf_op jit(solution)/shard_map/pack/pallas_call | solution.py:82
  11.0 16.3 %all_gather.3 = bf16[512,768]{1,0:T(8,128)(2,1)S(1)} all-gather(bf16[64,768]{1,0:T(8,128)(2,1)} %pack.1), channel_id=1, replica_groups=mesh['c'=4,'y'=4,'x'=4,'z'=4,'k'=2] {'z','k'}, dimensions={0}, use_global_device_ids=true | all-gather | bytes 884736 | tf_op jit(solution)/shard_map/all_gather | solution.py:263
  27.4 1.9 %collective-permute-start.2 = (bf16[768,256]{1,0:T(8,128)(2,1)S(1)}, bf16[768,256]{1,0:T(8,128)(2,1)S(1)}, u32[]{:S(2)}, u32[]{:S(2)}) collective-permute-start(bf16[768,256]{1,0:T(8,128)(2,1)S(1)} %pad_maximum_fusion.2), channel_id=1, source_target_pairs={{0,24},{1,97},{2,26},{3,99},{4,28},{5,101},{6,30},{7,103},{8,16},{... | collective-permute-start | bytes 1179656 | tf_op jit(solution)/shard_map/ppermute | solution.py:32
  29.3 1.9 %collective-permute-start.3 = (bf16[768,256]{1,0:T(8,128)(2,1)S(1)}, bf16[768,256]{1,0:T(8,128)(2,1)S(1)}, u32[]{:S(2)}, u32[]{:S(2)}) collective-permute-start(bf16[768,256]{1,0:T(8,128)(2,1)S(1)} %pad_maximum_fusion.2), channel_id=1, source_target_pairs={{0,16},{1,65},{2,18},{3,67},{4,20},{5,69},{6,22},{7,71},{8,24},{9,... | collective-permute-start | bytes 1179656 | tf_op jit(solution)/shard_map/ppermute | solution.py:32
  31.2 5.1 %collective-permute-start.1 = (bf16[768,256]{1,0:T(8,128)(2,1)S(1)}, bf16[768,256]{1,0:T(8,128)(2,1)S(1)}, u32[]{:S(2)}, u32[]{:S(2)}) collective-permute-start(bf16[768,256]{1,0:T(8,128)(2,1)S(1)} %pad_maximum_fusion.2), channel_id=1, source_target_pairs={{0,8},{1,33},{2,10},{3,35},{4,12},{5,37},{6,14},{7,39},{8,0},{9,41... | collective-permute-start | bytes 1179656 | tf_op jit(solution)/shard_map/ppermute | solution.py:32
  36.4 5.2 %collective-permute-done.2 = bf16[768,256]{1,0:T(8,128)(2,1)S(1)} collective-permute-done((bf16[768,256]{1,0:T(8,128)(2,1)S(1)}, bf16[768,256]{1,0:T(8,128)(2,1)S(1)}, u32[]{:S(2)}, u32[]{:S(2)}) %collective-permute-start.2) | collective-permute-done | bytes 393248 | tf_op jit(solution)/shard_map/ppermute | solution.py:32
  41.6 0.0 collective-permute-done.3
  41.6 0.1 pad_maximum_fusion.1.refs_3_
  41.7 1.9 %collective-permute-start.5 = (bf16[2,768,256]{2,1,0:T(8,128)(2,1)S(1)}, bf16[2,768,256]{2,1,0:T(8,128)(2,1)S(1)}, u32[]{:S(2)}, u32[]{:S(2)}) collective-permute-start(bf16[2,768,256]{2,1,0:T(8,128)(2,1)S(1)} %pad_maximum_fusion.1.refs_3_), channel_id=1, source_target_pairs={{0,96},{1,25},{2,98},{3,27},{4,100},{5,29},{6,102},{7,31},{8,104},... | collective-permute-start | bytes 2359304 | tf_op jit(solution)/shard_map/ppermute | solution.py:32
  43.6 0.5 collective-permute-done.1
  44.1 0.1 pad_maximum_fusion.refs_2_
  44.2 1.9 %collective-permute-start.4 = (bf16[2,768,256]{2,1,0:T(8,128)(2,1)S(1)}, bf16[2,768,256]{2,1,0:T(8,128)(2,1)S(1)}, u32[]{:S(2)}, u32[]{:S(2)}) collective-permute-start(bf16[2,768,256]{2,1,0:T(8,128)(2,1)S(1)} %pad_maximum_fusion.refs_2_), channel_id=1, source_target_pairs={{0,32},{1,9},{2,34},{3,11},{4,36},{5,13},{6,38},{7,15},{8,40},{9,1... | collective-permute-start | bytes 2359304 | tf_op jit(solution)/shard_map/ppermute | solution.py:32
  46.1 3.4 %collective-permute-start.6 = (bf16[2,768,256]{2,1,0:T(8,128)(2,1)S(1)}, bf16[2,768,256]{2,1,0:T(8,128)(2,1)}, u32[]{:S(2)}, u32[]{:S(2)}) collective-permute-start(bf16[2,768,256]{2,1,0:T(8,128)(2,1)S(1)} %pad_maximum_fusion.1.refs_3_), channel_id=1, source_target_pairs={{0,32},{1,9},{2,34},{3,11},{4,36},{5,13},{6,38},{7,15},{8,40},{9,1... | collective-permute-start | bytes 2359304 | tf_op jit(solution)/shard_map/ppermute | solution.py:32
  49.5 4.1 %collective-permute-start.7 = (bf16[2,768,256]{2,1,0:T(8,128)(2,1)S(1)}, bf16[2,768,256]{2,1,0:T(8,128)(2,1)}, u32[]{:S(2)}, u32[]{:S(2)}) collective-permute-start(bf16[2,768,256]{2,1,0:T(8,128)(2,1)S(1)} %pad_maximum_fusion.refs_2_), channel_id=1, source_target_pairs={{0,96},{1,25},{2,98},{3,27},{4,100},{5,29},{6,102},{7,31},{8,104},... | collective-permute-start | bytes 2359304 | tf_op jit(solution)/shard_map/ppermute | solution.py:32
  53.6 0.1 pad_add_fusion.at_ref
  53.7 2.2 %collective-permute-done.5.refs_5_ = bf16[2,768,256]{2,1,0:T(8,128)(2,1)S(1)} collective-permute-done((bf16[2,768,256]{2,1,0:T(8,128)(2,1)S(1)}, bf16[2,768,256]{2,1,0:T(8,128)(2,1)S(1)}, u32[]{:S(2)}, u32[]{:S(2)}) %collective-permute-start.5) | collective-permute-done | bytes 786464 | tf_op jit(solution)/shard_map/ppermute | solution.py:32
  55.9 1.9 %collective-permute-start.8 = (bf16[2,768,256]{2,1,0:T(8,128)(2,1)S(1)}, bf16[2,768,256]{2,1,0:T(8,128)(2,1)S(1)}, u32[]{:S(2)}, u32[]{:S(2)}) collective-permute-start(bf16[2,768,256]{2,1,0:T(8,128)(2,1)S(1)} %collective-permute-done.5.refs_5_), channel_id=1, source_target_pairs={{0,32},{1,9},{2,34},{3,11},{4,36},{5,13},{6,38},{7,15},{8,40},{9,1... | collective-permute-start | bytes 2359304 | tf_op jit(solution)/shard_map/ppermute | solution.py:32
  57.9 0.0 collective-permute-done.4.refs_4_
  57.9 3.6 %collective-permute-start.9 = (bf16[2,768,256]{2,1,0:T(8,128)(2,1)S(1)}, bf16[2,768,256]{2,1,0:T(8,128)(2,1)S(1)}, u32[]{:S(2)}, u32[]{:S(2)}) collective-permute-start(bf16[2,768,256]{2,1,0:T(8,128)(2,1)S(1)} %collective-permute-done.4.refs_4_), channel_id=1, source_target_pairs={{0,96},{1,25},{2,98},{3,27},{4,100},{5,29},{6,102},{7,31},{8,104},... | collective-permute-start | bytes 2359304 | tf_op jit(solution)/shard_map/ppermute | solution.py:32
  61.4 4.3 %collective-permute-done.6.refs_6_ = bf16[2,768,256]{2,1,0:T(8,128)(2,1)} collective-permute-done((bf16[2,768,256]{2,1,0:T(8,128)(2,1)S(1)}, bf16[2,768,256]{2,1,0:T(8,128)(2,1)}, u32[]{:S(2)}, u32[]{:S(2)}) %collective-permute-start.6) | collective-permute-done | bytes 786464 | tf_op jit(solution)/shard_map/ppermute | solution.py:32
  65.8 0.0 collective-permute-done.7.refs_7_
  65.8 0.0 collective-permute-done.refs_1_
  65.8 0.0 copy-start
  65.8 1.6 %copy-done = bf16[128,8192]{1,0:T(8,128)(2,1)S(1)} copy-done((bf16[128,8192]{1,0:T(8,128)(2,1)S(1)}, bf16[128,8192]{1,0:T(8,128)(2,1)}, u32[]{:S(2)}) %copy-start) | copy-done | bytes 2097176
  67.4 0.0 copy-start.1
  67.4 4.2 %early.1 = (f32[256,384]{1,0:T(8,128)S(1)}, bf16[6,2,256,256]{3,2,1,0:T(8,128)(2,1)S(1)}, bf16[2,2,256,512]{3,2,1,0:T(8,128)(2,1)S(1)}) custom-call(s32[49]{0:T(128)S(1)} %pad_add_fusion.at_ref, bf16[128,8192]{1,0:T(8,128)(2,1)S(1)} %copy-done, bf16[128,8192]{1,0:T(8,128)(2,1)} %collective-permute-done.refs_1_, ...), custom_call_target="tpu_custom_call" | custom-call | flops 6442450944 | bytes 6291456 | tf_op jit(solution)/shard_map/early/pallas_call | solution.py:177
  71.6 4.1 %collective-permute-start.10 = (bf16[6,2,256,256]{3,2,1,0:T(8,128)(2,1)S(1)}, bf16[6,2,256,256]{3,2,1,0:T(8,128)(2,1)S(1)}, u32[]{:S(2)}, u32[]{:S(2)}) collective-permute-start(bf16[6,2,256,256]{3,2,1,0:T(8,128)(2,1)S(1)} %get-tuple-element.8.own_early_ref), channel_id=1, source_target_pairs={{0,1},{1,0},{2,3},{3,2},{4,5},{5,4},{6,7},{7,6},{8,9},{9,8},{10,11... | collective-permute-start | bytes 4718600 | tf_op jit(solution)/shard_map/ppermute | solution.py:32
  75.6 0.0 copy-done.1
  75.7 7.1 %collective-permute-start.12 = (bf16[3,64,256]{2,1,0:T(8,128)(2,1)S(1)}, bf16[3,64,256]{2,1,0:T(8,128)(2,1)S(1)}, u32[]{:S(2)}, u32[]{:S(2)}) collective-permute-start(bf16[3,64,256]{2,1,0:T(8,128)(2,1)S(1)} %convert_element_type.18), channel_id=1, source_target_pairs={{0,128},{1,129},{2,130},{3,131},{4,132},{5,133},{6,134},{7,135},{8... | collective-permute-start | bytes 294920 | tf_op jit(solution)/shard_map/ppermute | solution.py:32
  82.8 0.0 collective-permute-done.8.refs_0_
  82.8 0.0 collective-permute-done.9.refs_1_
  82.8 0.5 late.1.own_late_ref
  83.3 2.2 %collective-permute-start.11 = (bf16[1152,256]{1,0:T(8,128)(2,1)S(1)}, bf16[1152,256]{1,0:T(8,128)(2,1)S(1)}, u32[]{:S(2)}, u32[]{:S(2)}) collective-permute-start(bf16[1152,256]{1,0:T(8,128)(2,1)S(1)} %late.1.own_late_ref), channel_id=1, source_target_pairs={{0,1},{1,0},{2,3},{3,2},{4,5},{5,4},{6,7},{7,6},{8,9},{9,8},{10,11... | collective-permute-start | bytes 1769480 | tf_op jit(solution)/shard_map/ppermute | solution.py:32
  85.5 6.8 %collective-permute-done.12 = bf16[3,64,256]{2,1,0:T(8,128)(2,1)S(1)} collective-permute-done((bf16[3,64,256]{2,1,0:T(8,128)(2,1)S(1)}, bf16[3,64,256]{2,1,0:T(8,128)(2,1)S(1)}, u32[]{:S(2)}, u32[]{:S(2)}) %collective-permute-start.12) | collective-permute-done | bytes 98336 | tf_op jit(solution)/shard_map/ppermute | solution.py:32
  92.4 6.7 %collective-permute-start.13 = (bf16[3,64,256]{2,1,0:T(8,128)(2,1)S(1)}, bf16[3,64,256]{2,1,0:T(8,128)(2,1)S(1)}, u32[]{:S(2)}, u32[]{:S(2)}) collective-permute-start(bf16[3,64,256]{2,1,0:T(8,128)(2,1)S(1)} %add_convert_fusion), channel_id=1, source_target_pairs={{0,384},{1,385},{2,386},{3,387},{4,388},{5,389},{6,390},{7,391},{8... | collective-permute-start | bytes 294920 | tf_op jit(solution)/shard_map/ppermute | solution.py:32
  99.1 7.3 %collective-permute-done.13 = bf16[3,64,256]{2,1,0:T(8,128)(2,1)S(1)} collective-permute-done((bf16[3,64,256]{2,1,0:T(8,128)(2,1)S(1)}, bf16[3,64,256]{2,1,0:T(8,128)(2,1)S(1)}, u32[]{:S(2)}, u32[]{:S(2)}) %collective-permute-start.13) | collective-permute-done | bytes 98336 | tf_op jit(solution)/shard_map/ppermute | solution.py:32
  106.4 0.7 add_multiply_fusion
  107.1 0.0 collective-permute-done.11.late_ref
  107.1 0.0 collective-permute-done.10.early_ref
  107.1 2.9 %down.1 = bf16[128,8192]{1,0:T(8,128)(2,1)} custom-call(s32[49]{0:T(128)S(1)} %pad_add_fusion.at_ref, bf16[6,2,256,256]{3,2,1,0:T(8,128)(2,1)S(1)} %get-tuple-element.8.own_early_ref, bf16[1152,256]{1,0:T(8,128)(2,1)S(1)} %late.1.own_late_ref, bf16[6,2,256,256]{3,2,1,0:T(8,128)(2,1)S(1)} %collective-permute-done.10.early_ref, ...), custom_call_target="tpu_custom_call" | custom-call | tf_op jit(solution)/shard_map/down/pallas_call | solution.py:245
  (7 shorter events, 0.1 us)
Async XLA Ops:
  0.6 65.1 %collective-permute-start = (bf16[128,8192]{1,0:T(8,128)(2,1)}, bf16[128,8192]{1,0:T(8,128)(2,1)}, u32[]{:S(2)}, u32[]{:S(2)}) collective-permute-start(bf16[128,8192]{1,0:T(8,128)(2,1)} %refs_0_.1), channel_id=1, source_target_pairs={{0,1},{1,0},{2,3},{3,2},{4,5},{5,4},{6,7},{7,6},{8,9},{9,8},{10,11... | collective-permute-start | bytes 6291464 | tf_op jit(solution)/shard_map/ppermute | solution.py:32
  27.4 14.2 %collective-permute-start.2 = (bf16[768,256]{1,0:T(8,128)(2,1)S(1)}, bf16[768,256]{1,0:T(8,128)(2,1)S(1)}, u32[]{:S(2)}, u32[]{:S(2)}) collective-permute-start(bf16[768,256]{1,0:T(8,128)(2,1)S(1)} %pad_maximum_fusion.2), channel_id=1, source_target_pairs={{0,24},{1,97},{2,26},{3,99},{4,28},{5,101},{6,30},{7,103},{8,16},{... | collective-permute-start | bytes 1179656 | tf_op jit(solution)/shard_map/ppermute | solution.py:32
  29.3 12.3 %collective-permute-start.3 = (bf16[768,256]{1,0:T(8,128)(2,1)S(1)}, bf16[768,256]{1,0:T(8,128)(2,1)S(1)}, u32[]{:S(2)}, u32[]{:S(2)}) collective-permute-start(bf16[768,256]{1,0:T(8,128)(2,1)S(1)} %pad_maximum_fusion.2), channel_id=1, source_target_pairs={{0,16},{1,65},{2,18},{3,67},{4,20},{5,69},{6,22},{7,71},{8,24},{9,... | collective-permute-start | bytes 1179656 | tf_op jit(solution)/shard_map/ppermute | solution.py:32
  31.2 12.9 %collective-permute-start.1 = (bf16[768,256]{1,0:T(8,128)(2,1)S(1)}, bf16[768,256]{1,0:T(8,128)(2,1)S(1)}, u32[]{:S(2)}, u32[]{:S(2)}) collective-permute-start(bf16[768,256]{1,0:T(8,128)(2,1)S(1)} %pad_maximum_fusion.2), channel_id=1, source_target_pairs={{0,8},{1,33},{2,10},{3,35},{4,12},{5,37},{6,14},{7,39},{8,0},{9,41... | collective-permute-start | bytes 1179656 | tf_op jit(solution)/shard_map/ppermute | solution.py:32
  41.7 14.2 %collective-permute-start.5 = (bf16[2,768,256]{2,1,0:T(8,128)(2,1)S(1)}, bf16[2,768,256]{2,1,0:T(8,128)(2,1)S(1)}, u32[]{:S(2)}, u32[]{:S(2)}) collective-permute-start(bf16[2,768,256]{2,1,0:T(8,128)(2,1)S(1)} %pad_maximum_fusion.1.refs_3_), channel_id=1, source_target_pairs={{0,96},{1,25},{2,98},{3,27},{4,100},{5,29},{6,102},{7,31},{8,104},... | collective-permute-start | bytes 2359304 | tf_op jit(solution)/shard_map/ppermute | solution.py:32
  44.2 13.7 %collective-permute-start.4 = (bf16[2,768,256]{2,1,0:T(8,128)(2,1)S(1)}, bf16[2,768,256]{2,1,0:T(8,128)(2,1)S(1)}, u32[]{:S(2)}, u32[]{:S(2)}) collective-permute-start(bf16[2,768,256]{2,1,0:T(8,128)(2,1)S(1)} %pad_maximum_fusion.refs_2_), channel_id=1, source_target_pairs={{0,32},{1,9},{2,34},{3,11},{4,36},{5,13},{6,38},{7,15},{8,40},{9,1... | collective-permute-start | bytes 2359304 | tf_op jit(solution)/shard_map/ppermute | solution.py:32
  46.1 19.6 %collective-permute-start.6 = (bf16[2,768,256]{2,1,0:T(8,128)(2,1)S(1)}, bf16[2,768,256]{2,1,0:T(8,128)(2,1)}, u32[]{:S(2)}, u32[]{:S(2)}) collective-permute-start(bf16[2,768,256]{2,1,0:T(8,128)(2,1)S(1)} %pad_maximum_fusion.1.refs_3_), channel_id=1, source_target_pairs={{0,32},{1,9},{2,34},{3,11},{4,36},{5,13},{6,38},{7,15},{8,40},{9,1... | collective-permute-start | bytes 2359304 | tf_op jit(solution)/shard_map/ppermute | solution.py:32
  49.5 16.3 %collective-permute-start.7 = (bf16[2,768,256]{2,1,0:T(8,128)(2,1)S(1)}, bf16[2,768,256]{2,1,0:T(8,128)(2,1)}, u32[]{:S(2)}, u32[]{:S(2)}) collective-permute-start(bf16[2,768,256]{2,1,0:T(8,128)(2,1)S(1)} %pad_maximum_fusion.refs_2_), channel_id=1, source_target_pairs={{0,96},{1,25},{2,98},{3,27},{4,100},{5,29},{6,102},{7,31},{8,104},... | collective-permute-start | bytes 2359304 | tf_op jit(solution)/shard_map/ppermute | solution.py:32
  55.9 26.8 %collective-permute-start.8 = (bf16[2,768,256]{2,1,0:T(8,128)(2,1)S(1)}, bf16[2,768,256]{2,1,0:T(8,128)(2,1)S(1)}, u32[]{:S(2)}, u32[]{:S(2)}) collective-permute-start(bf16[2,768,256]{2,1,0:T(8,128)(2,1)S(1)} %collective-permute-done.5.refs_5_), channel_id=1, source_target_pairs={{0,32},{1,9},{2,34},{3,11},{4,36},{5,13},{6,38},{7,15},{8,40},{9,1... | collective-permute-start | bytes 2359304 | tf_op jit(solution)/shard_map/ppermute | solution.py:32
  57.9 24.9 %collective-permute-start.9 = (bf16[2,768,256]{2,1,0:T(8,128)(2,1)S(1)}, bf16[2,768,256]{2,1,0:T(8,128)(2,1)S(1)}, u32[]{:S(2)}, u32[]{:S(2)}) collective-permute-start(bf16[2,768,256]{2,1,0:T(8,128)(2,1)S(1)} %collective-permute-done.4.refs_4_), channel_id=1, source_target_pairs={{0,96},{1,25},{2,98},{3,27},{4,100},{5,29},{6,102},{7,31},{8,104},... | collective-permute-start | bytes 2359304 | tf_op jit(solution)/shard_map/ppermute | solution.py:32
  65.8 1.6 %copy-start = (bf16[128,8192]{1,0:T(8,128)(2,1)S(1)}, bf16[128,8192]{1,0:T(8,128)(2,1)}, u32[]{:S(2)}) copy-start(bf16[128,8192]{1,0:T(8,128)(2,1)} %refs_0_.1) | copy-start | bytes 6291460
  67.4 8.3 %copy-start.1 = (f32[1,3,64,256]{3,2,1,0:T(8,128)S(1)}, f32[1,3,64,256]{3,2,1,0:T(8,128)}, u32[]{:S(2)}) copy-start(f32[1,3,64,256]{3,2,1,0:T(8,128)} %param.11) | copy-start | bytes 589828
  71.6 35.6 %collective-permute-start.10 = (bf16[6,2,256,256]{3,2,1,0:T(8,128)(2,1)S(1)}, bf16[6,2,256,256]{3,2,1,0:T(8,128)(2,1)S(1)}, u32[]{:S(2)}, u32[]{:S(2)}) collective-permute-start(bf16[6,2,256,256]{3,2,1,0:T(8,128)(2,1)S(1)} %get-tuple-element.8.own_early_ref), channel_id=1, source_target_pairs={{0,1},{1,0},{2,3},{3,2},{4,5},{5,4},{6,7},{7,6},{8,9},{9,8},{10,11... | collective-permute-start | bytes 4718600 | tf_op jit(solution)/shard_map/ppermute | solution.py:32
  75.7 16.7 %collective-permute-start.12 = (bf16[3,64,256]{2,1,0:T(8,128)(2,1)S(1)}, bf16[3,64,256]{2,1,0:T(8,128)(2,1)S(1)}, u32[]{:S(2)}, u32[]{:S(2)}) collective-permute-start(bf16[3,64,256]{2,1,0:T(8,128)(2,1)S(1)} %convert_element_type.18), channel_id=1, source_target_pairs={{0,128},{1,129},{2,130},{3,131},{4,132},{5,133},{6,134},{7,135},{8... | collective-permute-start | bytes 294920 | tf_op jit(solution)/shard_map/ppermute | solution.py:32
  83.3 23.8 %collective-permute-start.11 = (bf16[1152,256]{1,0:T(8,128)(2,1)S(1)}, bf16[1152,256]{1,0:T(8,128)(2,1)S(1)}, u32[]{:S(2)}, u32[]{:S(2)}) collective-permute-start(bf16[1152,256]{1,0:T(8,128)(2,1)S(1)} %late.1.own_late_ref), channel_id=1, source_target_pairs={{0,1},{1,0},{2,3},{3,2},{4,5},{5,4},{6,7},{7,6},{8,9},{9,8},{10,11... | collective-permute-start | bytes 1769480 | tf_op jit(solution)/shard_map/ppermute | solution.py:32
  92.4 14.0 %collective-permute-start.13 = (bf16[3,64,256]{2,1,0:T(8,128)(2,1)S(1)}, bf16[3,64,256]{2,1,0:T(8,128)(2,1)S(1)}, u32[]{:S(2)}, u32[]{:S(2)}) collective-permute-start(bf16[3,64,256]{2,1,0:T(8,128)(2,1)S(1)} %add_convert_fusion), channel_id=1, source_target_pairs={{0,384},{1,385},{2,386},{3,387},{4,388},{5,389},{6,390},{7,391},{8... | collective-permute-start | bytes 294920 | tf_op jit(solution)/shard_map/ppermute | solution.py:32
